TPU v7x, 128 devices: a whole 4x4x4 slice. The times are simulated.
128 devices in a mesh: row: 8 (over y_hi, z), col: 16 (over x, y_lo, core).
Axes of the slice: x: 4, y: 4 (y_hi: 2, y_lo: 2; y = y_hi * 2 + y_lo), z: 4, core: 2. Of those that a mesh axis runs over, the one named last changes fastest.
Arguments:
- response_coeffs: float32 [3, 8192, 1024], P(None, ('row', 'col')), may hold values from -6 to 6
- occupied_coeffs: float32 [8192, 1024], P(('row', 'col')), may hold values from -0.1875 to 0.1875
Outputs:
- density: float32 [3, 8192, 8192], P(None, 'row', 'col')
All inputs are finite; a program needn't handle non-finite values.
Results may differ from a plain program's by a relative error of at most 0.0003.
Values sent between devices are 32-bit elements; how exact they have to be, the bound alone decides.
No kernel may reach another device: no remote copies, remote signals or barrier semaphores. Data moves between devices by JAX's collectives and lax.ppermute only.
A program may use at most 128 MiB of HBM per device.

v0:
```python
import jax
import jax.numpy as jnp
from jax import lax
from jax.sharding import PartitionSpec as P

SLICE_PAIRS = ((0, 0), (0, 1), (1, 0))


def broadcast(value, axis, source):
    kept = jnp.where(lax.axis_index(axis) == source, value, 0).astype(value.dtype)
    return lax.psum(kept, axis)


def split_slices(values):
    leading = lax.optimization_barrier(values.astype(jnp.bfloat16))
    remainder = values - leading.astype(jnp.float32)
    trailing = lax.optimization_barrier(remainder.astype(jnp.bfloat16))
    return [leading, trailing]


def contribute(row_slices, column_slices, perturbations):
    accumulated = jnp.zeros(
        (perturbations, row_slices[0].shape[1], column_slices[0].shape[1]), jnp.float32
    )
    for left_index, right_index in SLICE_PAIRS:
        forward_term = jnp.einsum(
            "kro,co->krc",
            row_slices[left_index][:perturbations],
            column_slices[right_index][perturbations],
            preferred_element_type=jnp.float32,
        )
        mirror_term = jnp.einsum(
            "ro,kco->krc",
            row_slices[right_index][perturbations],
            column_slices[left_index][:perturbations],
            preferred_element_type=jnp.float32,
        )
        accumulated = accumulated + forward_term + mirror_term
    return accumulated


def shards(response_coeffs, occupied_coeffs):
    perturbations = response_coeffs.shape[0]
    stacked = jnp.concatenate([response_coeffs, occupied_coeffs[None]], axis=0)
    col_index = lax.axis_index("col")
    row_panel = lax.all_gather(stacked, "col", axis=1, tiled=True)
    half_rows = row_panel.shape[1] // 2
    own_half = lax.dynamic_slice_in_dim(row_panel, col_index % 2 * half_rows, half_rows, 1)
    column_panel = broadcast(own_half, "row", col_index // 2)
    density = contribute(split_slices(row_panel), split_slices(column_panel), perturbations)
    return density


def solution(mesh):
    return jax.shard_map(
        shards,
        mesh=mesh,
        in_specs=(P(None, ("row", "col"), None), P(("row", "col"), None)),
        out_specs=P(None, "row", "col"),
        check_vma=False,
    )
```

profile of v0, /device:TPU:1, one launch (start us, length us, event | category | flops | bytes accessed | tf_op | source)
XLA Modules:
  0.0 361.2 jit_solution(1945731837348868768)
XLA Ops:
  6.5 0.0 all-gather.2.cloned.1.call-start
  6.5 2.3 pad_maximum_fusion
  8.8 0.0 all-gather.2.cloned.1.call-update
  8.9 0.0 all-reduce.2.cloned.1.call-start
  8.9 95.2 %all-gather.2.cloned.1.call-done = f32[4,1024,1024]{2,1,0:T(8,128)} async-done(((f32[4,64,1024]{2,1,0:T(8,128)}), f32[4,1024,1024]{2,1,0:T(8,128)}) %all-gather.2.cloned.1.call-update) | async-done | bytes 16777232 | tf_op jit(solution)/shard_map/all_gather | solution.py:46
  104.2 8.5 %dynamic-slice_select_fusion = f32[4,512,1024]{2,1,0:T(8,128)} fusion(f32[4,1024,1024]{2,1,0:T(8,128)} %all-gather.2.cloned.1.call-done, s32[]{:T(128)S(6)} %select_n.25, pred[]{:T(512)S(6)} %eq.5), kind=kLoop, calls=%fused_computation.2 | loop fusion | flops 2097152 | bytes 16777220 | tf_op jit(solution)/shard_map/jit(_where)/select_n | solution.py:10
  112.7 0.0 all-reduce.2.cloned.1.call-update
  112.7 6.6 %convert_element_type.20 = bf16[4,1024,1024]{2,1,0:T(8,128)(2,1)S(1)} convert(f32[4,1024,1024]{2,1,0:T(8,128)} %all-gather.2.cloned.1.call-done) | non-fusion elementwise | flops 4194304 | bytes 25165824 | tf_op jit(solution)/shard_map/convert_element_type | solution.py:15
  119.3 0.0 copy-start
  119.3 3.5 copy-done
  122.8 10.2 %subtract_convert_fusion = bf16[4,1024,1024]{2,1,0:T(8,128)(2,1)} fusion(f32[4,1024,1024]{2,1,0:T(8,128)} %all-gather.2.cloned.1.call-done, bf16[4,1024,1024]{2,1,0:T(8,128)(2,1)S(1)} %convert_element_type.20), kind=kLoop, calls=%fused_computation | loop fusion | flops 12582912 | bytes 33554432 | tf_op jit(solution)/shard_map/convert_element_type | solution.py:17
  133.0 166.2 %all-reduce.2.cloned.1.call-done = f32[4,512,1024]{2,1,0:T(8,128)} async-done(((f32[4,512,1024]{2,1,0:T(8,128)}), f32[4,512,1024]{2,1,0:T(8,128)}) %all-reduce.2.cloned.1.call-update) | async-done | bytes 8388624 | tf_op jit(solution)/shard_map/psum | solution.py:11
  299.1 0.0 copy-start.2
  299.1 4.2 %convert_element_type.21 = bf16[4,512,1024]{2,1,0:T(8,128)(2,1)S(1)} convert(f32[4,512,1024]{2,1,0:T(8,128)} %all-reduce.2.cloned.1.call-done) | non-fusion elementwise | flops 2097152 | bytes 12582912 | tf_op jit(solution)/shard_map/convert_element_type | solution.py:15
  303.4 1.6 copy-done.2
  304.9 0.0 copy-start.1
  304.9 0.0 slice-start
  304.9 5.4 %fusion.5 = f32[3,1024,512]{2,1,0:T(8,128)} fusion(bf16[4,1024,1024]{2,1,0:T(8,128)(2,1)S(1)} %copy-done.2, bf16[4,512,1024]{2,1,0:T(8,128)(2,1)S(1)} %convert_element_type.21), kind=kOutput, calls=%fused_computation.16 | convolution fusion | flops 3221225472 | bytes 15728640 | tf_op jit(solution)/shard_map/kro,co->krc/dot_general | solution.py:26
  310.3 0.0 slice-start.1
  310.3 7.2 %fusion.2 = f32[3,512,1024]{1,2,0:T(8,128)} fusion(bf16[4,512,1024]{2,1,0:T(8,128)(2,1)S(1)} %convert_element_type.21, bf16[4,1024,1024]{2,1,0:T(8,128)(2,1)} %subtract_convert_fusion), kind=kOutput, calls=%fused_computation.9 | convolution fusion | flops 3221225472 | bytes 12582912 | tf_op jit(solution)/shard_map/ro,kco->krc/dot_general | solution.py:32
  317.5 0.0 slice-done
  317.5 0.0 slice-done.1
  317.5 5.5 %fusion.6 = f32[3,1024,512]{2,1,0:T(8,128)} fusion(bf16[4,1024,1024]{2,1,0:T(8,128)(2,1)S(1)} %bitcast.40, bf16[4,512,1024]{2,1,0:T(8,128)(2,1)S(1)} %convert_element_type.21), kind=kOutput, calls=%fused_computation.17 | convolution fusion | flops 3221225472 | bytes 15728640 | tf_op jit(solution)/shard_map/kro,co->krc/dot_general | solution.py:26
  323.0 0.0 copy-done.1
  323.0 5.4 %fusion.3 = f32[3,512,1024]{1,2,0:T(8,128)} fusion(bf16[4,512,1024]{2,1,0:T(8,128)(2,1)S(1)} %convert_element_type.21, bf16[4,1024,1024]{2,1,0:T(8,128)(2,1)S(1)} %bitcast.40), kind=kOutput, calls=%fused_computation.11 | convolution fusion | flops 3221225472 | bytes 12582912 | tf_op jit(solution)/shard_map/ro,kco->krc/dot_general | solution.py:32
  328.4 6.2 %subtract_convert_fusion.1 = bf16[4,512,1024]{2,1,0:T(8,128)(2,1)S(1)} fusion(f32[4,512,1024]{2,1,0:T(8,128)} %all-reduce.2.cloned.1.call-done, bf16[4,512,1024]{2,1,0:T(8,128)(2,1)} %copy-done.1), kind=kLoop, calls=%fused_computation.1 | loop fusion | flops 6291456 | bytes 16777216 | tf_op jit(solution)/shard_map/convert_element_type | solution.py:17
  334.6 5.4 %fusion.4 = f32[3,1024,512]{2,1,0:T(8,128)} fusion(bf16[4,1024,1024]{2,1,0:T(8,128)(2,1)S(1)} %bitcast.40, bf16[4,512,1024]{2,1,0:T(8,128)(2,1)S(1)} %subtract_convert_fusion.1), kind=kOutput, calls=%fused_computation.13 | convolution fusion | flops 3221225472 | bytes 15728640 | tf_op jit(solution)/shard_map/kro,co->krc/dot_general | solution.py:26
  340.0 14.3 %bitcast_add_fusion = f32[3,1024,512]{2,1,0:T(8,128)} fusion(f32[3,1024,512]{2,1,0:T(8,128)} %fusion.5, f32[3,512,1024]{1,2,0:T(8,128)} %fusion.2, f32[3,1024,512]{2,1,0:T(8,128)} %fusion.4, f32[3,1024,512]{2,1,0:T(8,128)} %fusion.6, f32[3,512,1024]{1,2,0:T(8,128)} %fusion.3, bf16[4,512,1024]{2,1,0:T(8,128)(2,1)S(1)} %subtract_convert_fusion.1, ...), kind=kOutput, calls=%fused_computation.3 | convolution fusion | flops 3229089792 | bytes 44040192 | tf_op jit(solution)/shard_map/ro,kco->krc/dot_general | solution.py:32
  (1 shorter events, 0.0 us)
Async XLA Ops:
  6.5 97.6 %all-gather.2.cloned.1.call-start = ((), (), s32[]{:S(2)}) async-start(), calls=%async_computation | async-start | bytes 17825792 | tf_op jit(solution)/shard_map/all_gather | solution.py:46
  8.9 290.3 %all-reduce.2.cloned.1.call-start = ((), (), s32[]{:S(2)}) async-start(), calls=%async_computation.1 | async-start | bytes 16777216 | tf_op jit(solution)/shard_map/psum | solution.py:11
  119.3 3.5 copy-start
  299.1 5.8 %copy-start.2 = (bf16[4,1024,1024]{2,1,0:T(8,128)(2,1)S(1)}, bf16[4,1024,1024]{2,1,0:T(8,128)(2,1)}, u32[]{:S(2)}) copy-start(bf16[4,1024,1024]{2,1,0:T(8,128)(2,1)} %subtract_convert_fusion) | copy-start | bytes 25165828
  304.9 18.1 %copy-start.1 = (bf16[4,512,1024]{2,1,0:T(8,128)(2,1)}, bf16[4,512,1024]{2,1,0:T(8,128)(2,1)S(1)}, u32[]{:S(2)}) copy-start(bf16[4,512,1024]{2,1,0:T(8,128)(2,1)S(1)} %convert_element_type.21) | copy-start | bytes 12582916
  304.9 12.6 %slice-start = ((s8[8388608]{0:T(1024)(128)(4,1)}), s8[4194304]{0:T(1024)(128)(4,1)S(1)}, s32[]{:S(2)}) async-start(s8[8388608]{0:T(1024)(128)(4,1)} %bitcast.39), calls=%async_computation.2 | async-start | bytes 8388608
  310.3 7.2 %slice-start.1 = ((s8[8388608]{0:T(1024)(128)(4,1)}), s8[4194304]{0:T(1024)(128)(4,1)S(1)}, s32[]{:S(2)}) async-start(s8[8388608]{0:T(1024)(128)(4,1)} %bitcast.39), calls=%async_computation.3 | async-start | bytes 8388608
Sparse Core Ops, SparseCore 0:
  9.0 95.1 all-gather.1
  112.8 186.2 all-reduce.1
where the time goes:
time: 361 us
  waiting for transfers between devices  261 us (72%)
  matrix products  43.2 us (12%)
  other arithmetic  38 us (11%)
  between operations  13.5 us (4%)
  local copies, waits for them, and re-layouts  5.1 us (1%)
    psum x1, waiting for transfers between devices, broadcast(): return lax.psum(kept, axis)  166 us
    all_gather x1, waiting for transfers between devices, shards(): row_panel = lax.all_gather(stacked, 'col', axis=1, tiled=True)  95.2 us
    dot_general x3, matrix products, contribute(): jnp.einsum('ro,kco->krc', row_slices[right_index][perturbations], column_...  27 us
    convert_element_type x2, other arithmetic, split_slices(): trailing = lax.optimization_barrier(remainder.astype(jnp.bfloat16))  16.4 us
    dot_general x3, matrix products, contribute(): jnp.einsum('kro,co->krc', row_slices[left_index][:perturbations], column_...  16.3 us
    convert_element_type x2, other arithmetic, split_slices(): leading = lax.optimization_barrier(values.astype(jnp.bfloat16))  10.8 us
    select_n x1, other arithmetic, broadcast(): jnp.where(lax.axis_index(axis) == source, value, 0).astype(value.dtype)  8.5 us
  transfers between devices with their start and end apart: 2, of which 2 were waited for; matrix products, arithmetic and copies ran while one was open for 5% of the time, Pallas kernels for 0%

commit v1 on v0

v1 whole, which is shorter than its diff:
```python
import functools

import jax
import jax.numpy as jnp
from jax import lax
from jax.experimental import pallas as pl
from jax.experimental.pallas import tpu as pltpu
from jax.sharding import PartitionSpec as P


AXES = ("row", "col")
PIECES = ((0, 512), (512, 512))


def place(index):
    row, col = divmod(index, 16)
    y_hi, z = divmod(row, 4)
    x, rest = divmod(col, 4)
    y_lo, core = divmod(rest, 2)
    return x, y_hi, y_lo, z, core


def index_of(x, y_hi, y_lo, z, core):
    return (y_hi % 2 * 4 + z % 4) * 16 + x % 4 * 4 + y_lo % 2 * 2 + core % 2


def move(value, target):
    pairs = [(source, index_of(*target(*place(source)))) for source in range(128)]
    return lax.ppermute(value, AXES, pairs)


def gather_rows(own):
    step_x = lambda d: lambda x, h, l, z, k: (x + d, h, l, z, k)
    pair = move(own, lambda x, h, l, z, k: (x, h, l + 1, z, k))
    own_minus = move(own, step_x(1))
    own_plus = move(own, step_x(-1))
    pair_minus = move(pair, step_x(1))
    pair_plus = move(pair, step_x(-1))
    own_far = move(own_minus, step_x(1))
    pair_far = move(pair_plus, step_x(-1))
    chunks = (own, pair, own_minus, pair_minus, own_plus, pair_plus, own_far, pair_far)
    swap = lambda x, h, l, z, k: (x, h, l, z, k + 1)
    return [(chunk, move(chunk, swap)) for chunk in chunks]


def gather_columns(own):
    step_z = lambda d: lambda x, h, l, z, k: (x, h, l, z + d, k)
    shifted = move(own, lambda x, h, l, z, k: (x, h, l, z + 2 * k + l, k))

    def into_column(x, h, l, z, k):
        source = (z - 2 * k - l) % 4
        return 2 * h + source // 2, x % 2, source % 2, z, x // 2

    entry = move(shifted, into_column)
    other = move(entry, lambda x, h, l, z, k: (x, h + 1, l, z, k))
    entry_minus = move(entry, step_z(1))
    entry_plus = move(entry, step_z(-1))
    other_minus = move(other, step_z(1))
    other_plus = move(other, step_z(-1))
    entry_far = move(entry_minus, step_z(1))
    other_far = move(other_plus, step_z(-1))
    return (
        (entry, entry_minus, entry_plus, entry_far),
        (other, other_minus, other_plus, other_far),
    )


OFFSETS = (0, 3, 1, 2)
CALLS = (((0, 2), (2, 4)), ((0, 2), (2, 4)))


def split(value):
    high = value.astype(jnp.bfloat16)
    low = (value - high.astype(jnp.float32)).astype(jnp.bfloat16)
    return high, low


def density_kernel(add, tiles, tile_ref, within_ref, slot_ref, *refs):
    rows, columns, refs = refs[: 4 * tiles], refs[4 * tiles : 4 * tiles + 8], refs[4 * tiles + 8 :]
    if add is not None:
        before, refs = refs[0], refs[1:]
    out, row_full, col_full, row_high, row_low, col_high, col_low, held, made = refs[:9]
    row_sem, col_sem, held_sem, made_sem = refs[9:]
    _, mats, height, depth = row_full.shape
    count, last = 4 * height, mats - 1

    def block(ref, t):
        start = pl.multiple_of(tile_ref[t] * count, count)
        return ref.at[:, pl.ds(start, count), :]

    def fetch_rows(i, source):
        return pltpu.make_async_copy(source, row_full.at[i], row_sem.at[i])

    def fetch_held(t):
        return pltpu.make_async_copy(block(before, t), held.at[t], held_sem.at[t])

    def store(t):
        slot = lax.rem(t, 2)
        return pltpu.make_async_copy(made.at[slot], block(out, t), made_sem.at[slot])

    copies = []
    for n, column in enumerate(columns):
        copies.append(pltpu.make_async_copy(column, col_full.at[n], col_sem.at[n]))
        copies[-1].start()
    for t in range(tiles):
        for i in range(4 * t, 4 * t + 4):
            fetch_rows(i, rows[i]).start()
        if add:
            fetch_held(t).start()
    for n, copy in enumerate(copies):
        copy.wait()
        slot = slot_ref[n]
        high, low = split(col_full[n])
        col_high[:, slot] = high
        col_low[:, slot] = low

    dims = (((1,), (1,)), ((), ()))
    dot = lambda u, v: lax.dot_general(u, v, dims, preferred_element_type=jnp.float32)
    row = lambda ref, k: ref[k].reshape(count, depth)
    col = lambda ref, k: ref[k].reshape(8 * height, depth)

    def step(t, carry):
        for n in range(4):
            i = 4 * t + n
            fetch_rows(i, rows[n]).wait()
            high, low = split(row_full[i])
            row_high[:, n ^ within_ref[0]] = high
            row_low[:, n ^ within_ref[0]] = low
        if add:
            fetch_held(t).wait()

        @pl.when(t >= 2)
        def _():
            store(t - 2).wait()

        for k in range(last):
            total = (
                dot(row(row_high, k), col(col_high, last))
                + dot(row(row_high, last), col(col_high, k))
                + dot(row(row_high, k), col(col_low, last))
                + dot(row(row_low, k), col(col_high, last))
                + dot(row(row_high, last), col(col_low, k))
                + dot(row(row_low, last), col(col_high, k))
            )
            if add:
                total = total + held[t, k]
            made[lax.rem(t, 2), k] = total
        store(t).start()
        return carry

    lax.fori_loop(0, tiles, step, 0)
    for t in range(max(tiles - 2, 0), tiles):
        store(t).wait()


def add_tiles(rows, columns, where, within, slots, before, add):
    tiles = len(rows) // 4
    mats, height, depth = rows[0].shape
    count, width = 4 * height, 8 * height
    operands = [*rows, *columns]
    if before is None:
        add = None
    else:
        operands.append(before)
    vmem = lambda shape, dtype: pltpu.VMEM(shape, dtype)
    return pl.pallas_call(
        functools.partial(density_kernel, add, tiles),
        out_shape=jax.ShapeDtypeStruct((mats - 1, 4 * count, width), jnp.float32),
        grid_spec=pltpu.PrefetchScalarGridSpec(
            num_scalar_prefetch=3,
            grid=(1,),
            in_specs=[pl.BlockSpec(memory_space=pltpu.HBM)] * len(operands),
            out_specs=pl.BlockSpec(memory_space=pltpu.HBM),
            scratch_shapes=[
                vmem((4 * tiles, mats, height, depth), jnp.float32),
                vmem((8, mats, height, depth), jnp.float32),
                vmem((mats, 4, height, depth), jnp.bfloat16),
                vmem((mats, 4, height, depth), jnp.bfloat16),
                vmem((mats, 8, height, depth), jnp.bfloat16),
                vmem((mats, 8, height, depth), jnp.bfloat16),
                vmem((tiles if add else 1, mats - 1, count, width), jnp.float32),
                vmem((2, mats - 1, count, width), jnp.float32),
                pltpu.SemaphoreType.DMA((4 * tiles,)),
                pltpu.SemaphoreType.DMA((8,)),
                pltpu.SemaphoreType.DMA((4,)),
                pltpu.SemaphoreType.DMA((2,)),
            ],
        ),
        input_output_aliases={} if before is None else {2 + len(operands): 0},
        cost_estimate=pl.CostEstimate(
            flops=2 * 6 * (mats - 1) * tiles * count * width * depth,
            bytes_accessed=(len(rows) + 8) * mats * height * depth * 4,
            transcendentals=0,
        ),
    )(where, within, slots, *operands)


def whole(response_coeffs, occupied_coeffs):
    own = jnp.concatenate([response_coeffs, occupied_coeffs[None]], axis=0)
    row, col = lax.axis_index("row"), lax.axis_index("col")
    x, pair = col // 4, col % 4
    y_hi, z = row // 4, row % 4
    source = (x % 2) * 2 + pair // 2
    parts = [own[:, :, s : s + d] for s, d in PIECES]
    columns = [gather_columns(part) for part in parts]
    tiles = [gather_rows(part) for part in parts]
    turn = (z + jnp.array(OFFSETS) - source) % 4
    base = turn % 2 * 2 + turn // 2
    slots = jnp.concatenate([y_hi * 4 + base, (1 - y_hi) * 4 + base]).astype(jnp.int32)
    where = ((x + jnp.array(OFFSETS)) % 4).astype(jnp.int32)
    within = pair[None].astype(jnp.int32)
    density = None
    for n, (entry, other) in enumerate(columns):
        for start, stop in CALLS[n]:
            rows = sum(tiles[n][2 * start : 2 * stop], ())
            density = add_tiles(
                rows,
                (*entry, *other),
                where[start:stop],
                within,
                slots,
                density,
                n > 0,
            )
    return density


def solution(mesh):
    return jax.shard_map(
        whole,
        mesh=mesh,
        in_specs=(P(None, ("row", "col"), None), P(("row", "col"), None)),
        out_specs=P(None, "row", "col"),
        check_vma=False,
    )
```

time: 361 us -> 218 us (0.60)
  waiting for transfers between devices: 261 us -> 66.6 us
  starting transfers between devices: 0.04 us -> 96.7 us
  Pallas kernels: 0 us -> 46.1 us
  matrix products: 43.2 us -> 0 us
  other arithmetic: 38 us -> 2.63 us
  between operations: 13.5 us -> 0.62 us
    psum x1 -> x0, waiting for transfers between devices: 166 us -> none  [broadcast(): return lax.psum(kept, axis)]
    ppermute x0 -> x48, starting transfers between devices: none -> 96.7 us  [move(): return lax.ppermute(value, AXES, pairs)]
    all_gather x1 -> x0, waiting for transfers between devices: 95.2 us -> none  [shards(): row_panel = lax.all_gather(stacked, 'col', axis=1, tiled=True)]
    ppermute x0 -> x48, waiting for transfers between devices: none -> 66.6 us  [move(): return lax.ppermute(value, AXES, pairs)]
    pallas_call x0 -> x4, Pallas kernels: none -> 46.1 us  [add_tiles(): pl.pallas_call(functools.partial(density_kernel, add, tiles), out_shape=j...]
    dot_general x6 -> x0, matrix products: 43.2 us -> none  [the longest x3 27 us: contribute(): jnp.einsum('ro,kco->krc', row_slices[right_index][perturbations], column_...]
    convert_element_type x4 -> x0, other arithmetic: 27.2 us -> none  [the longest x2 16.4 us: split_slices(): trailing = lax.optimization_barrier(remainder.astype(jnp.bfloat16))]
    select_n x1 -> x0, other arithmetic: 8.5 us -> none  [broadcast(): jnp.where(lax.axis_index(axis) == source, value, 0).astype(value.dtype)]
  transfers between devices with their start and end apart: 2 -> 48, of which waited for: 2 -> 16; matrix products, arithmetic and copies ran while one was open for 5% -> 1% of each run, Pallas kernels for 0% -> 16%
where the time goes in v1:
time: 218 us; the launch traced here: 216 us
  starting transfers between devices  96.7 us (44%)
  waiting for transfers between devices  66.6 us (31%)
  Pallas kernels  46.1 us (21%)
  local copies, waits for them, and re-layouts  3.84 us (2%)
  other arithmetic  2.63 us (1%)
    ppermute x48, starting transfers between devices, move(): return lax.ppermute(value, AXES, pairs)  96.7 us
    ppermute x48, waiting for transfers between devices, move(): return lax.ppermute(value, AXES, pairs)  66.6 us
    pallas_call x4, Pallas kernels, add_tiles(): pl.pallas_call(functools.partial(density_kernel, add, tiles), out_shape=j...  46.1 us
  transfers between devices with their start and end apart: 48, of which 16 were waited for; matrix products, arithmetic and copies ran while one was open for 1% of the time, Pallas kernels for 16%

profile of v1, /device:TPU:1, one launch (start us, length us, event | category | flops | bytes accessed | tf_op | source)
XLA Modules:
  0.0 216.5 jit_solution(9293143854860308281)
XLA Ops:
  0.0 1.3 pad_maximum_fusion
  1.3 6.3 %collective-permute-start.34 = (f32[4,64,512]{2,1,0:T(8,128)S(1)}, f32[4,64,512]{2,1,0:T(8,128)S(1)}, u32[]{:S(2)}, u32[]{:S(2)}) collective-permute-start(f32[4,64,512]{2,1,0:T(8,128)S(1)} %get-tuple-element.7.refs_0_), channel_id=1, source_target_pairs={{0,0},{1,33},{2,18},{3,51},{4,4},{5,37},{6,22},{7,55},{8,8},{9,41}... | collective-permute-start | bytes 1572872 | tf_op jit(solution)/shard_map/ppermute | solution.py:29
  7.7 1.5 collective-permute-start.26
  9.2 1.2 collective-permute-start.29
  10.4 1.5 collective-permute-start.24
  11.9 2.3 %collective-permute-done.34 = f32[4,64,512]{2,1,0:T(8,128)S(1)} collective-permute-done((f32[4,64,512]{2,1,0:T(8,128)S(1)}, f32[4,64,512]{2,1,0:T(8,128)S(1)}, u32[]{:S(2)}, u32[]{:S(2)}) %collective-permute-start.34) | collective-permute-done | bytes 524320 | tf_op jit(solution)/shard_map/ppermute | solution.py:29
  14.2 5.1 %collective-permute-start.10 = (f32[4,64,512]{2,1,0:T(8,128)S(1)}, f32[4,64,512]{2,1,0:T(8,128)S(1)}, u32[]{:S(2)}, u32[]{:S(2)}) collective-permute-start(f32[4,64,512]{2,1,0:T(8,128)S(1)} %get-tuple-element.8.refs_0_), channel_id=1, source_target_pairs={{0,0},{1,33},{2,18},{3,51},{4,4},{5,37},{6,22},{7,55},{8,8},{9,41}... | collective-permute-start | bytes 1572872 | tf_op jit(solution)/shard_map/ppermute | solution.py:29
  19.4 1.3 collective-permute-done.26.refs_2_
  20.7 1.7 collective-permute-start.2
  22.5 1.2 collective-permute-done.29.refs_4_
  23.6 0.3 collective-permute-start.5
  23.9 0.2 collective-permute-start.19
  24.2 0.6 copy-done.31
  24.8 2.4 %collective-permute-start = (f32[4,64,512]{2,1,0:T(8,128)S(1)}, f32[4,64,512]{2,1,0:T(8,128)S(1)}, u32[]{:S(2)}, u32[]{:S(2)}) collective-permute-start(f32[4,64,512]{2,1,0:T(8,128)S(1)} %get-tuple-element.8.refs_0_), channel_id=1, source_target_pairs={{0,12},{1,13},{2,14},{3,15},{4,0},{5,1},{6,2},{7,3},{8,4},{9,5},{1... | collective-permute-start | bytes 1572872 | tf_op jit(solution)/shard_map/ppermute | solution.py:29
  27.1 1.9 collective-permute-start.35
  29.1 5.7 %collective-permute-done.2.refs_2_ = f32[4,64,512]{2,1,0:T(8,128)S(1)} collective-permute-done((f32[4,64,512]{2,1,0:T(8,128)S(1)}, f32[4,64,512]{2,1,0:T(8,128)S(1)}, u32[]{:S(2)}, u32[]{:S(2)}) %collective-permute-start.2) | collective-permute-done | bytes 524320 | tf_op jit(solution)/shard_map/ppermute | solution.py:29
  34.8 1.2 collective-permute-start.46
  36.0 2.1 collective-permute-done.5.refs_4_
  38.1 1.2 collective-permute-start.44
  39.4 1.9 collective-permute-start.27
  41.3 7.7 %collective-permute-done.35.refs_8_ = f32[4,64,512]{2,1,0:T(8,128)S(1)} collective-permute-done((f32[4,64,512]{2,1,0:T(8,128)S(1)}, f32[4,64,512]{2,1,0:T(8,128)S(1)}, u32[]{:S(2)}, u32[]{:S(2)}) %collective-permute-start.35) | collective-permute-done | bytes 524320 | tf_op jit(solution)/shard_map/ppermute | solution.py:29
  49.0 7.1 %collective-permute-start.30 = (f32[4,64,512]{2,1,0:T(8,128)S(1)}, f32[4,64,512]{2,1,0:T(8,128)S(1)}, u32[]{:S(2)}, u32[]{:S(2)}) collective-permute-start(f32[4,64,512]{2,1,0:T(8,128)S(1)} %collective-permute-done.29.refs_4_), channel_id=1, source_target_pairs={{0,4},{1,5},{2,6},{3,7},{4,8},{5,9},{6,10},{7,11},{8,12},{9,13},{1... | collective-permute-start | bytes 1572872 | tf_op jit(solution)/shard_map/ppermute | solution.py:29
  56.0 0.1 collective-permute-done.46.refs_6_
  56.1 11.1 %collective-permute-start.25 = (f32[4,64,512]{2,1,0:T(8,128)S(1)}, f32[4,64,512]{2,1,0:T(8,128)}, u32[]{:S(2)}, u32[]{:S(2)}) collective-permute-start(f32[4,64,512]{2,1,0:T(8,128)S(1)} %collective-permute-done.24.refs_0_), channel_id=1, source_target_pairs={{0,1},{1,0},{2,3},{3,2},{4,5},{5,4},{6,7},{7,6},{8,9},{9,8},{10,11... | collective-permute-start | bytes 1572872 | tf_op jit(solution)/shard_map/ppermute | solution.py:29
  67.3 1.9 collective-permute-start.11
  69.3 0.6 collective-permute-start.22
  70.0 2.9 %collective-permute-start.21 = (f32[4,64,512]{2,1,0:T(8,128)S(1)}, f32[4,64,512]{2,1,0:T(8,128)S(1)}, u32[]{:S(2)}, u32[]{:S(2)}) collective-permute-start(f32[4,64,512]{2,1,0:T(8,128)S(1)} %collective-permute-done.5.refs_4_), channel_id=1, source_target_pairs={{0,1},{1,0},{2,3},{3,2},{4,5},{5,4},{6,7},{7,6},{8,9},{9,8},{10,11... | collective-permute-start | bytes 1572872 | tf_op jit(solution)/shard_map/ppermute | solution.py:29
  72.9 11.5 %collective-permute-done.11.refs_8_ = f32[4,64,512]{2,1,0:T(8,128)S(1)} collective-permute-done((f32[4,64,512]{2,1,0:T(8,128)S(1)}, f32[4,64,512]{2,1,0:T(8,128)S(1)}, u32[]{:S(2)}, u32[]{:S(2)}) %collective-permute-start.11) | collective-permute-done | bytes 524320 | tf_op jit(solution)/shard_map/ppermute | solution.py:29
  84.4 5.8 %collective-permute-done.22.refs_6_ = f32[4,64,512]{2,1,0:T(8,128)S(1)} collective-permute-done((f32[4,64,512]{2,1,0:T(8,128)S(1)}, f32[4,64,512]{2,1,0:T(8,128)S(1)}, u32[]{:S(2)}, u32[]{:S(2)}) %collective-permute-start.22) | collective-permute-done | bytes 524320 | tf_op jit(solution)/shard_map/ppermute | solution.py:29
  90.2 0.9 collective-permute-start.39
  91.1 0.8 collective-permute-start.36
  91.9 5.8 %collective-permute-start.37 = (f32[4,64,512]{2,1,0:T(8,128)S(1)}, f32[4,64,512]{2,1,0:T(8,128)S(1)}, u32[]{:S(2)}, u32[]{:S(2)}) collective-permute-start(f32[4,64,512]{2,1,0:T(8,128)S(1)} %collective-permute-done.35.refs_8_), channel_id=1, source_target_pairs={{0,48},{1,49},{2,50},{3,51},{4,52},{5,53},{6,54},{7,55},{8,56},{9,... | collective-permute-start | bytes 1572872 | tf_op jit(solution)/shard_map/ppermute | solution.py:29
  97.7 5.8 %collective-permute-start.47 = (f32[4,64,512]{2,1,0:T(8,128)S(1)}, f32[4,64,512]{2,1,0:T(8,128)S(1)}, u32[]{:S(2)}, u32[]{:S(2)}) collective-permute-start(f32[4,64,512]{2,1,0:T(8,128)S(1)} %collective-permute-done.46.refs_6_), channel_id=1, source_target_pairs={{0,1},{1,0},{2,3},{3,2},{4,5},{5,4},{6,7},{7,6},{8,9},{9,8},{10,11... | collective-permute-start | bytes 1572872 | tf_op jit(solution)/shard_map/ppermute | solution.py:29
  103.5 7.4 %collective-permute-start.28 = (f32[4,64,512]{2,1,0:T(8,128)S(1)}, f32[4,64,512]{2,1,0:T(8,128)S(1)}, u32[]{:S(2)}, u32[]{:S(2)}) collective-permute-start(f32[4,64,512]{2,1,0:T(8,128)S(1)} %collective-permute-done.27.refs_2_), channel_id=1, source_target_pairs={{0,1},{1,0},{2,3},{3,2},{4,5},{5,4},{6,7},{7,6},{8,9},{9,8},{10,11... | collective-permute-start | bytes 1572872 | tf_op jit(solution)/shard_map/ppermute | solution.py:29
  111.1 2.8 %collective-permute-start.15 = (f32[4,64,512]{2,1,0:T(8,128)S(1)}, f32[4,64,512]{2,1,0:T(8,128)S(1)}, u32[]{:S(2)}, u32[]{:S(2)}) collective-permute-start(f32[4,64,512]{2,1,0:T(8,128)S(1)} %collective-permute-done.11.refs_8_), channel_id=1, source_target_pairs={{0,64},{1,65},{2,66},{3,67},{4,68},{5,69},{6,70},{7,71},{8,72},{9,... | collective-permute-start | bytes 1572872 | tf_op jit(solution)/shard_map/ppermute | solution.py:29
  114.0 0.4 collective-permute-done.32.refs_6_
  114.5 3.1 %collective-permute-start.13 = (f32[4,64,512]{2,1,0:T(8,128)S(1)}, f32[4,64,512]{2,1,0:T(8,128)S(1)}, u32[]{:S(2)}, u32[]{:S(2)}) collective-permute-start(f32[4,64,512]{2,1,0:T(8,128)S(1)} %collective-permute-done.11.refs_8_), channel_id=1, source_target_pairs={{0,48},{1,49},{2,50},{3,51},{4,52},{5,53},{6,54},{7,55},{8,56},{9,... | collective-permute-start | bytes 1572872 | tf_op jit(solution)/shard_map/ppermute | solution.py:29
  117.8 0.6 copy-done.23
  118.4 1.5 collective-permute-start.23
  119.9 5.8 %collective-permute-done.15.refs_12_ = f32[4,64,512]{2,1,0:T(8,128)S(1)} collective-permute-done((f32[4,64,512]{2,1,0:T(8,128)S(1)}, f32[4,64,512]{2,1,0:T(8,128)S(1)}, u32[]{:S(2)}, u32[]{:S(2)}) %collective-permute-start.15) | collective-permute-done | bytes 524320 | tf_op jit(solution)/shard_map/ppermute | solution.py:29
  125.7 2.7 %collective-permute-done.12.refs_9_ = f32[4,64,512]{2,1,0:T(8,128)S(1)} collective-permute-done((f32[4,64,512]{2,1,0:T(8,128)S(1)}, f32[4,64,512]{2,1,0:T(8,128)S(1)}, u32[]{:S(2)}, u32[]{:S(2)}) %collective-permute-start.12) | collective-permute-done | bytes 524320 | tf_op jit(solution)/shard_map/ppermute | solution.py:29
  128.4 0.2 collective-permute-done.13.refs_10_
  128.6 3.4 %collective-permute-start.17 = (f32[4,64,512]{2,1,0:T(8,128)S(1)}, f32[4,64,512]{2,1,0:T(8,128)S(1)}, u32[]{:S(2)}, u32[]{:S(2)}) collective-permute-start(f32[4,64,512]{2,1,0:T(8,128)S(1)} %collective-permute-done.15.refs_12_), channel_id=1, source_target_pairs={{0,48},{1,49},{2,50},{3,51},{4,52},{5,53},{6,54},{7,55},{8,56},{9,... | collective-permute-start | bytes 1572872 | tf_op jit(solution)/shard_map/ppermute | solution.py:29
  132.0 0.7 broadcast_add_fusion.1
  132.6 7.2 %collective-permute-done.41.refs_14_ = f32[4,64,512]{2,1,0:T(8,128)} collective-permute-done((f32[4,64,512]{2,1,0:T(8,128)}, f32[4,64,512]{2,1,0:T(8,128)}, u32[]{:S(2)}, u32[]{:S(2)}) %collective-permute-start.41) | collective-permute-done | bytes 524320 | tf_op jit(solution)/shard_map/ppermute | solution.py:29
  139.9 3.4 %collective-permute-start.42 = (f32[4,64,512]{2,1,0:T(8,128)}, f32[4,64,512]{2,1,0:T(8,128)}, u32[]{:S(2)}, u32[]{:S(2)}) collective-permute-start(f32[4,64,512]{2,1,0:T(8,128)} %collective-permute-done.41.refs_14_), channel_id=1, source_target_pairs={{0,48},{1,49},{2,50},{3,51},{4,52},{5,53},{6,54},{7,55},{8,56},{9,... | collective-permute-start | bytes 1572872 | tf_op jit(solution)/shard_map/ppermute | solution.py:29
  143.3 0.7 fusion.6
  144.0 1.2 collective-permute-start.8
  145.3 5.4 %collective-permute-done.38.refs_11_ = f32[4,64,512]{2,1,0:T(8,128)} collective-permute-done((f32[4,64,512]{2,1,0:T(8,128)}, f32[4,64,512]{2,1,0:T(8,128)}, u32[]{:S(2)}, u32[]{:S(2)}) %collective-permute-start.38) | collective-permute-done | bytes 524320 | tf_op jit(solution)/shard_map/ppermute | solution.py:29
  150.7 3.9 %collective-permute-start.33 = (f32[4,64,512]{2,1,0:T(8,128)}, f32[4,64,512]{2,1,0:T(8,128)}, u32[]{:S(2)}, u32[]{:S(2)}) collective-permute-start(f32[4,64,512]{2,1,0:T(8,128)} %copy-done.22), channel_id=1, source_target_pairs={{0,1},{1,0},{2,3},{3,2},{4,5},{5,4},{6,7},{7,6},{8,9},{9,8},{10,11... | collective-permute-start | bytes 1572872 | tf_op jit(solution)/shard_map/ppermute | solution.py:29
  154.6 0.6 pad_add_fusion.slot_ref
  155.2 7.2 %collective-permute-done.42.refs_15_ = f32[4,64,512]{2,1,0:T(8,128)} collective-permute-done((f32[4,64,512]{2,1,0:T(8,128)}, f32[4,64,512]{2,1,0:T(8,128)}, u32[]{:S(2)}, u32[]{:S(2)}) %collective-permute-start.42) | collective-permute-done | bytes 524320 | tf_op jit(solution)/shard_map/ppermute | solution.py:29
  162.4 3.4 %collective-permute-start.18 = (f32[4,64,512]{2,1,0:T(8,128)S(1)}, f32[4,64,512]{2,1,0:T(8,128)}, u32[]{:S(2)}, u32[]{:S(2)}) collective-permute-start(f32[4,64,512]{2,1,0:T(8,128)S(1)} %collective-permute-done.17.refs_14_), channel_id=1, source_target_pairs={{0,48},{1,49},{2,50},{3,51},{4,52},{5,53},{6,54},{7,55},{8,56},{9,... | collective-permute-start | bytes 1572872 | tf_op jit(solution)/shard_map/ppermute | solution.py:29
  165.8 11.3 %shard_map.46.refs_16_ = f32[3,1024,512]{2,1,0:T(8,128)} custom-call(s32[2]{0:T(128)} %get-tuple-element.9.tile_ref, s32[1]{0:T(128)} %bitcast.within_ref, s32[8]{0:T(128)} %pad_add_fusion.slot_ref, f32[4,64,512]{2,1,0:T(8,128)} %copy-done.28, f32[4,64,512]{2,1,0:T(8,128)} %copy-done.31, f32[4,64,512]{2,1,0:T(8,128)} %copy-done.29, ...), custom_call_target="tpu_custom_call" | custom-call | flops 4831838208 | bytes 8388608 | tf_op jit(solution)/shard_map/pallas_call | solution.py:166
  177.1 1.5 collective-permute-start.1
  178.8 0.4 collective-permute-start.7
  179.2 0.3 collective-permute-start.9
  179.5 11.3 %shard_map.47.refs_16_ = f32[3,1024,512]{2,1,0:T(8,128)} custom-call(s32[2]{0:T(128)} %get-tuple-element.10.tile_ref, s32[1]{0:T(128)} %bitcast.within_ref, s32[8]{0:T(128)} %pad_add_fusion.slot_ref, f32[4,64,512]{2,1,0:T(8,128)} %copy-done.10, f32[4,64,512]{2,1,0:T(8,128)} %collective-permute-done.25.refs_1_, ...), custom_call_target="tpu_custom_call", output_to_operand_aliasing={{}: (19, {})} | custom-call | flops 4831838208 | bytes 8388608 | tf_op jit(solution)/shard_map/pallas_call | solution.py:166
  190.8 11.8 %shard_map.48.refs_16_ = f32[3,1024,512]{2,1,0:T(8,128)} custom-call(s32[2]{0:T(128)} %get-tuple-element.9.tile_ref, s32[1]{0:T(128)} %bitcast.within_ref, s32[8]{0:T(128)} %pad_add_fusion.slot_ref, f32[4,64,512]{2,1,0:T(8,128)} %copy-done.6, f32[4,64,512]{2,1,0:T(8,128)} %copy-done.11, f32[4,64,512]{2,1,0:T(8,128)} %copy-done.8, ...), custom_call_target="tpu_custom_call", output_to_operand_aliasing={{}: (19, {})} | custom-call | flops 4831838208 | bytes 8388608 | tf_op jit(solution)/shard_map/pallas_call | solution.py:166
  202.6 0.8 copy-done.24
  203.4 0.2 copy-done.25
  203.6 0.2 copy-done.26
  203.7 0.8 copy-done.27
  204.5 11.7 %shard_map.49 = f32[3,1024,512]{2,1,0:T(8,128)} custom-call(s32[2]{0:T(128)} %get-tuple-element.10.tile_ref, s32[1]{0:T(128)} %bitcast.within_ref, s32[8]{0:T(128)} %pad_add_fusion.slot_ref, f32[4,64,512]{2,1,0:T(8,128)} %copy-done.7, f32[4,64,512]{2,1,0:T(8,128)} %copy-done.24, f32[4,64,512]{2,1,0:T(8,128)} %copy-done.15, ...), custom_call_target="tpu_custom_call", output_to_operand_aliasing={{}: (19, {})} | custom-call | flops 4831838208 | bytes 8388608 | tf_op jit(solution)/shard_map/pallas_call | solution.py:166
  (113 shorter events, 0.8 us)
Async XLA Ops:
  1.3 112.7 %copy-start.6 = (f32[4,64,512]{2,1,0:T(8,128)}, f32[4,64,512]{2,1,0:T(8,128)S(1)}, u32[]{:S(2)}) copy-start(f32[4,64,512]{2,1,0:T(8,128)S(1)} %get-tuple-element.8.refs_0_) | copy-start | bytes 1572868
  1.3 12.9 %collective-permute-start.34 = (f32[4,64,512]{2,1,0:T(8,128)S(1)}, f32[4,64,512]{2,1,0:T(8,128)S(1)}, u32[]{:S(2)}, u32[]{:S(2)}) collective-permute-start(f32[4,64,512]{2,1,0:T(8,128)S(1)} %get-tuple-element.7.refs_0_), channel_id=1, source_target_pairs={{0,0},{1,33},{2,18},{3,51},{4,4},{5,37},{6,22},{7,55},{8,8},{9,41}... | collective-permute-start | bytes 1572872 | tf_op jit(solution)/shard_map/ppermute | solution.py:29
  7.7 13.0 %collective-permute-start.26 = (f32[4,64,512]{2,1,0:T(8,128)S(1)}, f32[4,64,512]{2,1,0:T(8,128)S(1)}, u32[]{:S(2)}, u32[]{:S(2)}) collective-permute-start(f32[4,64,512]{2,1,0:T(8,128)S(1)} %get-tuple-element.7.refs_0_), channel_id=1, source_target_pairs={{0,2},{1,3},{2,0},{3,1},{4,6},{5,7},{6,4},{7,5},{8,10},{9,11},{10,... | collective-permute-start | bytes 1572872 | tf_op jit(solution)/shard_map/ppermute | solution.py:29
  9.2 14.4 %collective-permute-start.29 = (f32[4,64,512]{2,1,0:T(8,128)S(1)}, f32[4,64,512]{2,1,0:T(8,128)S(1)}, u32[]{:S(2)}, u32[]{:S(2)}) collective-permute-start(f32[4,64,512]{2,1,0:T(8,128)S(1)} %get-tuple-element.7.refs_0_), channel_id=1, source_target_pairs={{0,4},{1,5},{2,6},{3,7},{4,8},{5,9},{6,10},{7,11},{8,12},{9,13},{1... | collective-permute-start | bytes 1572872 | tf_op jit(solution)/shard_map/ppermute | solution.py:29
  10.4 13.5 %collective-permute-start.43 = (f32[4,64,512]{2,1,0:T(8,128)S(1)}, f32[4,64,512]{2,1,0:T(8,128)S(1)}, u32[]{:S(2)}, u32[]{:S(2)}) collective-permute-start(f32[4,64,512]{2,1,0:T(8,128)S(1)} %get-tuple-element.7.refs_0_), channel_id=1, source_target_pairs={{0,1},{1,0},{2,3},{3,2},{4,5},{5,4},{6,7},{7,6},{8,9},{9,8},{10,11... | collective-permute-start | bytes 1572872 | tf_op jit(solution)/shard_map/ppermute | solution.py:29
  10.4 14.3 %collective-permute-start.24 = (f32[4,64,512]{2,1,0:T(8,128)S(1)}, f32[4,64,512]{2,1,0:T(8,128)S(1)}, u32[]{:S(2)}, u32[]{:S(2)}) collective-permute-start(f32[4,64,512]{2,1,0:T(8,128)S(1)} %get-tuple-element.7.refs_0_), channel_id=1, source_target_pairs={{0,12},{1,13},{2,14},{3,15},{4,0},{5,1},{6,2},{7,3},{8,4},{9,5},{1... | collective-permute-start | bytes 1572872 | tf_op jit(solution)/shard_map/ppermute | solution.py:29
  14.2 12.9 %collective-permute-start.10 = (f32[4,64,512]{2,1,0:T(8,128)S(1)}, f32[4,64,512]{2,1,0:T(8,128)S(1)}, u32[]{:S(2)}, u32[]{:S(2)}) collective-permute-start(f32[4,64,512]{2,1,0:T(8,128)S(1)} %get-tuple-element.8.refs_0_), channel_id=1, source_target_pairs={{0,0},{1,33},{2,18},{3,51},{4,4},{5,37},{6,22},{7,55},{8,8},{9,41}... | collective-permute-start | bytes 1572872 | tf_op jit(solution)/shard_map/ppermute | solution.py:29
  20.7 49.1 %copy-start.29 = (f32[4,64,512]{2,1,0:T(8,128)}, f32[4,64,512]{2,1,0:T(8,128)S(1)}, u32[]{:S(2)}) copy-start(f32[4,64,512]{2,1,0:T(8,128)S(1)} %collective-permute-done.26.refs_2_) | copy-start | bytes 1572868
  20.7 14.1 %collective-permute-start.2 = (f32[4,64,512]{2,1,0:T(8,128)S(1)}, f32[4,64,512]{2,1,0:T(8,128)S(1)}, u32[]{:S(2)}, u32[]{:S(2)}) collective-permute-start(f32[4,64,512]{2,1,0:T(8,128)S(1)} %get-tuple-element.8.refs_0_), channel_id=1, source_target_pairs={{0,2},{1,3},{2,0},{3,1},{4,6},{5,7},{6,4},{7,5},{8,10},{9,11},{10,... | collective-permute-start | bytes 1572872 | tf_op jit(solution)/shard_map/ppermute | solution.py:29
  23.6 46.3 %copy-start.30 = (f32[4,64,512]{2,1,0:T(8,128)}, f32[4,64,512]{2,1,0:T(8,128)S(1)}, u32[]{:S(2)}) copy-start(f32[4,64,512]{2,1,0:T(8,128)S(1)} %collective-permute-done.29.refs_4_) | copy-start | bytes 1572868
  23.6 14.4 %collective-permute-start.5 = (f32[4,64,512]{2,1,0:T(8,128)S(1)}, f32[4,64,512]{2,1,0:T(8,128)S(1)}, u32[]{:S(2)}, u32[]{:S(2)}) collective-permute-start(f32[4,64,512]{2,1,0:T(8,128)S(1)} %get-tuple-element.8.refs_0_), channel_id=1, source_target_pairs={{0,4},{1,5},{2,6},{3,7},{4,8},{5,9},{6,10},{7,11},{8,12},{9,13},{1... | collective-permute-start | bytes 1572872 | tf_op jit(solution)/shard_map/ppermute | solution.py:29
  23.9 15.3 %collective-permute-start.19 = (f32[4,64,512]{2,1,0:T(8,128)S(1)}, f32[4,64,512]{2,1,0:T(8,128)S(1)}, u32[]{:S(2)}, u32[]{:S(2)}) collective-permute-start(f32[4,64,512]{2,1,0:T(8,128)S(1)} %get-tuple-element.8.refs_0_), channel_id=1, source_target_pairs={{0,1},{1,0},{2,3},{3,2},{4,5},{5,4},{6,7},{7,6},{8,9},{9,8},{10,11... | collective-permute-start | bytes 1572872 | tf_op jit(solution)/shard_map/ppermute | solution.py:29
  24.8 89.7 %copy-start.10 = (f32[4,64,512]{2,1,0:T(8,128)}, f32[4,64,512]{2,1,0:T(8,128)S(1)}, u32[]{:S(2)}) copy-start(f32[4,64,512]{2,1,0:T(8,128)S(1)} %collective-permute-done.24.refs_0_) | copy-start | bytes 1572868
  24.8 14.6 %collective-permute-start = (f32[4,64,512]{2,1,0:T(8,128)S(1)}, f32[4,64,512]{2,1,0:T(8,128)S(1)}, u32[]{:S(2)}, u32[]{:S(2)}) collective-permute-start(f32[4,64,512]{2,1,0:T(8,128)S(1)} %get-tuple-element.8.refs_0_), channel_id=1, source_target_pairs={{0,12},{1,13},{2,14},{3,15},{4,0},{5,1},{6,2},{7,3},{8,4},{9,5},{1... | collective-permute-start | bytes 1572872 | tf_op jit(solution)/shard_map/ppermute | solution.py:29
  27.1 21.8 %collective-permute-start.35 = (f32[4,64,512]{2,1,0:T(8,128)S(1)}, f32[4,64,512]{2,1,0:T(8,128)S(1)}, u32[]{:S(2)}, u32[]{:S(2)}) collective-permute-start(f32[4,64,512]{2,1,0:T(8,128)S(1)} %collective-permute-done.34), channel_id=1, source_target_pairs={{0,0},{1,4},{2,6},{3,2},{4,64},{5,68},{6,70},{7,66},{8,1},{9,5},{1... | collective-permute-start | bytes 1572872 | tf_op jit(solution)/shard_map/ppermute | solution.py:29
  34.8 76.3 %copy-start.8 = (f32[4,64,512]{2,1,0:T(8,128)}, f32[4,64,512]{2,1,0:T(8,128)S(1)}, u32[]{:S(2)}) copy-start(f32[4,64,512]{2,1,0:T(8,128)S(1)} %collective-permute-done.2.refs_2_) | copy-start | bytes 1572868
  34.8 21.3 %collective-permute-start.46 = (f32[4,64,512]{2,1,0:T(8,128)S(1)}, f32[4,64,512]{2,1,0:T(8,128)S(1)}, u32[]{:S(2)}, u32[]{:S(2)}) collective-permute-start(f32[4,64,512]{2,1,0:T(8,128)S(1)} %collective-permute-done.26.refs_2_), channel_id=1, source_target_pairs={{0,4},{1,5},{2,6},{3,7},{4,8},{5,9},{6,10},{7,11},{8,12},{9,13},{1... | collective-permute-start | bytes 1572872 | tf_op jit(solution)/shard_map/ppermute | solution.py:29
  38.1 75.8 %copy-start.9 = (f32[4,64,512]{2,1,0:T(8,128)}, f32[4,64,512]{2,1,0:T(8,128)S(1)}, u32[]{:S(2)}) copy-start(f32[4,64,512]{2,1,0:T(8,128)S(1)} %collective-permute-done.5.refs_4_) | copy-start | bytes 1572868
  38.1 29.2 %collective-permute-start.44 = (f32[4,64,512]{2,1,0:T(8,128)S(1)}, f32[4,64,512]{2,1,0:T(8,128)S(1)}, u32[]{:S(2)}, u32[]{:S(2)}) collective-permute-start(f32[4,64,512]{2,1,0:T(8,128)S(1)} %collective-permute-done.26.refs_2_), channel_id=1, source_target_pairs={{0,1},{1,0},{2,3},{3,2},{4,5},{5,4},{6,7},{7,6},{8,9},{9,8},{10,11... | collective-permute-start | bytes 1572872 | tf_op jit(solution)/shard_map/ppermute | solution.py:29
  39.3 78.3 %copy-start.11 = (f32[4,64,512]{2,1,0:T(8,128)}, f32[4,64,512]{2,1,0:T(8,128)S(1)}, u32[]{:S(2)}) copy-start(f32[4,64,512]{2,1,0:T(8,128)S(1)} %collective-permute-done.19.refs_1_) | copy-start | bytes 1572868
  39.3 29.9 %collective-permute-start.45 = (f32[4,64,512]{2,1,0:T(8,128)S(1)}, f32[4,64,512]{2,1,0:T(8,128)S(1)}, u32[]{:S(2)}, u32[]{:S(2)}) collective-permute-start(f32[4,64,512]{2,1,0:T(8,128)S(1)} %collective-permute-done.29.refs_4_), channel_id=1, source_target_pairs={{0,1},{1,0},{2,3},{3,2},{4,5},{5,4},{6,7},{7,6},{8,9},{9,8},{10,11... | collective-permute-start | bytes 1572872 | tf_op jit(solution)/shard_map/ppermute | solution.py:29
  39.4 30.5 %collective-permute-start.27 = (f32[4,64,512]{2,1,0:T(8,128)S(1)}, f32[4,64,512]{2,1,0:T(8,128)S(1)}, u32[]{:S(2)}, u32[]{:S(2)}) collective-permute-start(f32[4,64,512]{2,1,0:T(8,128)S(1)} %collective-permute-done.26.refs_2_), channel_id=1, source_target_pairs={{0,12},{1,13},{2,14},{3,15},{4,0},{5,1},{6,2},{7,3},{8,4},{9,5},{1... | collective-permute-start | bytes 1572872 | tf_op jit(solution)/shard_map/ppermute | solution.py:29
  49.0 68.6 %copy-start.12 = (f32[4,64,512]{2,1,0:T(8,128)}, f32[4,64,512]{2,1,0:T(8,128)S(1)}, u32[]{:S(2)}) copy-start(f32[4,64,512]{2,1,0:T(8,128)S(1)} %collective-permute-done.35.refs_8_) | copy-start | bytes 1572868
  49.0 21.0 %collective-permute-start.30 = (f32[4,64,512]{2,1,0:T(8,128)S(1)}, f32[4,64,512]{2,1,0:T(8,128)S(1)}, u32[]{:S(2)}, u32[]{:S(2)}) collective-permute-start(f32[4,64,512]{2,1,0:T(8,128)S(1)} %collective-permute-done.29.refs_4_), channel_id=1, source_target_pairs={{0,4},{1,5},{2,6},{3,7},{4,8},{5,9},{6,10},{7,11},{8,12},{9,13},{1... | collective-permute-start | bytes 1572872 | tf_op jit(solution)/shard_map/ppermute | solution.py:29
  56.1 61.5 %copy-start.32 = (f32[4,64,512]{2,1,0:T(8,128)}, f32[4,64,512]{2,1,0:T(8,128)S(1)}, u32[]{:S(2)}) copy-start(f32[4,64,512]{2,1,0:T(8,128)S(1)} %collective-permute-done.46.refs_6_) | copy-start | bytes 1572868
  56.1 16.8 %collective-permute-start.25 = (f32[4,64,512]{2,1,0:T(8,128)S(1)}, f32[4,64,512]{2,1,0:T(8,128)}, u32[]{:S(2)}, u32[]{:S(2)}) collective-permute-start(f32[4,64,512]{2,1,0:T(8,128)S(1)} %collective-permute-done.24.refs_0_), channel_id=1, source_target_pairs={{0,1},{1,0},{2,3},{3,2},{4,5},{5,4},{6,7},{7,6},{8,9},{9,8},{10,11... | collective-permute-start | bytes 1572872 | tf_op jit(solution)/shard_map/ppermute | solution.py:29
  67.3 17.1 %collective-permute-start.11 = (f32[4,64,512]{2,1,0:T(8,128)S(1)}, f32[4,64,512]{2,1,0:T(8,128)S(1)}, u32[]{:S(2)}, u32[]{:S(2)}) collective-permute-start(f32[4,64,512]{2,1,0:T(8,128)S(1)} %collective-permute-done.10), channel_id=1, source_target_pairs={{0,0},{1,4},{2,6},{3,2},{4,64},{5,68},{6,70},{7,66},{8,1},{9,5},{1... | collective-permute-start | bytes 1572872 | tf_op jit(solution)/shard_map/ppermute | solution.py:29
  69.3 20.9 %collective-permute-start.22 = (f32[4,64,512]{2,1,0:T(8,128)S(1)}, f32[4,64,512]{2,1,0:T(8,128)S(1)}, u32[]{:S(2)}, u32[]{:S(2)}) collective-permute-start(f32[4,64,512]{2,1,0:T(8,128)S(1)} %collective-permute-done.2.refs_2_), channel_id=1, source_target_pairs={{0,4},{1,5},{2,6},{3,7},{4,8},{5,9},{6,10},{7,11},{8,12},{9,13},{1... | collective-permute-start | bytes 1572872 | tf_op jit(solution)/shard_map/ppermute | solution.py:29
  69.9 47.8 %copy-start.13 = (f32[4,64,512]{2,1,0:T(8,128)}, f32[4,64,512]{2,1,0:T(8,128)S(1)}, u32[]{:S(2)}) copy-start(f32[4,64,512]{2,1,0:T(8,128)S(1)} %collective-permute-done.27.refs_2_) | copy-start | bytes 1572868
  69.9 21.2 %collective-permute-start.20 = (f32[4,64,512]{2,1,0:T(8,128)S(1)}, f32[4,64,512]{2,1,0:T(8,128)S(1)}, u32[]{:S(2)}, u32[]{:S(2)}) collective-permute-start(f32[4,64,512]{2,1,0:T(8,128)S(1)} %collective-permute-done.2.refs_2_), channel_id=1, source_target_pairs={{0,1},{1,0},{2,3},{3,2},{4,5},{5,4},{6,7},{7,6},{8,9},{9,8},{10,11... | collective-permute-start | bytes 1572872 | tf_op jit(solution)/shard_map/ppermute | solution.py:29
  70.0 58.4 %copy-start.16 = (f32[4,64,512]{2,1,0:T(8,128)}, f32[4,64,512]{2,1,0:T(8,128)S(1)}, u32[]{:S(2)}) copy-start(f32[4,64,512]{2,1,0:T(8,128)S(1)} %collective-permute-done.30.refs_4_) | copy-start | bytes 1572868
  70.0 21.9 %collective-permute-start.21 = (f32[4,64,512]{2,1,0:T(8,128)S(1)}, f32[4,64,512]{2,1,0:T(8,128)S(1)}, u32[]{:S(2)}, u32[]{:S(2)}) collective-permute-start(f32[4,64,512]{2,1,0:T(8,128)S(1)} %collective-permute-done.5.refs_4_), channel_id=1, source_target_pairs={{0,1},{1,0},{2,3},{3,2},{4,5},{5,4},{6,7},{7,6},{8,9},{9,8},{10,11... | collective-permute-start | bytes 1572872 | tf_op jit(solution)/shard_map/ppermute | solution.py:29
  72.9 24.8 %collective-permute-start.3 = (f32[4,64,512]{2,1,0:T(8,128)S(1)}, f32[4,64,512]{2,1,0:T(8,128)S(1)}, u32[]{:S(2)}, u32[]{:S(2)}) collective-permute-start(f32[4,64,512]{2,1,0:T(8,128)S(1)} %collective-permute-done.2.refs_2_), channel_id=1, source_target_pairs={{0,12},{1,13},{2,14},{3,15},{4,0},{5,1},{6,2},{7,3},{8,4},{9,5},{1... | collective-permute-start | bytes 1572872 | tf_op jit(solution)/shard_map/ppermute | solution.py:29
  84.4 92.7 %copy-start = (f32[4,64,512]{2,1,0:T(8,128)}, f32[4,64,512]{2,1,0:T(8,128)S(1)}, u32[]{:S(2)}) copy-start(f32[4,64,512]{2,1,0:T(8,128)S(1)} %collective-permute-done.11.refs_8_) | copy-start | bytes 1572868
  84.4 19.1 %collective-permute-start.6 = (f32[4,64,512]{2,1,0:T(8,128)S(1)}, f32[4,64,512]{2,1,0:T(8,128)S(1)}, u32[]{:S(2)}, u32[]{:S(2)}) collective-permute-start(f32[4,64,512]{2,1,0:T(8,128)S(1)} %collective-permute-done.5.refs_4_), channel_id=1, source_target_pairs={{0,4},{1,5},{2,6},{3,7},{4,8},{5,9},{6,10},{7,11},{8,12},{9,13},{1... | collective-permute-start | bytes 1572872 | tf_op jit(solution)/shard_map/ppermute | solution.py:29
  90.2 55.0 %copy-start.14 = (f32[4,64,512]{2,1,0:T(8,128)}, f32[4,64,512]{2,1,0:T(8,128)S(1)}, u32[]{:S(2)}) copy-start(f32[4,64,512]{2,1,0:T(8,128)S(1)} %collective-permute-done.22.refs_6_) | copy-start | bytes 1572868
  90.2 13.4 %collective-permute-start.39 = (f32[4,64,512]{2,1,0:T(8,128)S(1)}, f32[4,64,512]{2,1,0:T(8,128)}, u32[]{:S(2)}, u32[]{:S(2)}) collective-permute-start(f32[4,64,512]{2,1,0:T(8,128)S(1)} %collective-permute-done.35.refs_8_), channel_id=1, source_target_pairs={{0,64},{1,65},{2,66},{3,67},{4,68},{5,69},{6,70},{7,71},{8,72},{9,... | collective-permute-start | bytes 1572872 | tf_op jit(solution)/shard_map/ppermute | solution.py:29
  91.1 19.9 %collective-permute-start.36 = (f32[4,64,512]{2,1,0:T(8,128)S(1)}, f32[4,64,512]{2,1,0:T(8,128)S(1)}, u32[]{:S(2)}, u32[]{:S(2)}) collective-permute-start(f32[4,64,512]{2,1,0:T(8,128)S(1)} %collective-permute-done.35.refs_8_), channel_id=1, source_target_pairs={{0,16},{1,17},{2,18},{3,19},{4,20},{5,21},{6,22},{7,23},{8,24},{9,... | collective-permute-start | bytes 1572872 | tf_op jit(solution)/shard_map/ppermute | solution.py:29
  91.9 19.2 %collective-permute-start.37 = (f32[4,64,512]{2,1,0:T(8,128)S(1)}, f32[4,64,512]{2,1,0:T(8,128)S(1)}, u32[]{:S(2)}, u32[]{:S(2)}) collective-permute-start(f32[4,64,512]{2,1,0:T(8,128)S(1)} %collective-permute-done.35.refs_8_), channel_id=1, source_target_pairs={{0,48},{1,49},{2,50},{3,51},{4,52},{5,53},{6,54},{7,55},{8,56},{9,... | collective-permute-start | bytes 1572872 | tf_op jit(solution)/shard_map/ppermute | solution.py:29
  97.7 16.2 %collective-permute-start.47 = (f32[4,64,512]{2,1,0:T(8,128)S(1)}, f32[4,64,512]{2,1,0:T(8,128)S(1)}, u32[]{:S(2)}, u32[]{:S(2)}) collective-permute-start(f32[4,64,512]{2,1,0:T(8,128)S(1)} %collective-permute-done.46.refs_6_), channel_id=1, source_target_pairs={{0,1},{1,0},{2,3},{3,2},{4,5},{5,4},{6,7},{7,6},{8,9},{9,8},{10,11... | collective-permute-start | bytes 1572872 | tf_op jit(solution)/shard_map/ppermute | solution.py:29
  103.5 10.9 %collective-permute-start.32 = (f32[4,64,512]{2,1,0:T(8,128)S(1)}, f32[4,64,512]{2,1,0:T(8,128)S(1)}, u32[]{:S(2)}, u32[]{:S(2)}) collective-permute-start(f32[4,64,512]{2,1,0:T(8,128)S(1)} %collective-permute-done.27.refs_2_), channel_id=1, source_target_pairs={{0,12},{1,13},{2,14},{3,15},{4,0},{5,1},{6,2},{7,3},{8,4},{9,5},{1... | collective-permute-start | bytes 1572872 | tf_op jit(solution)/shard_map/ppermute | solution.py:29
  103.5 14.0 %collective-permute-start.28 = (f32[4,64,512]{2,1,0:T(8,128)S(1)}, f32[4,64,512]{2,1,0:T(8,128)S(1)}, u32[]{:S(2)}, u32[]{:S(2)}) collective-permute-start(f32[4,64,512]{2,1,0:T(8,128)S(1)} %collective-permute-done.27.refs_2_), channel_id=1, source_target_pairs={{0,1},{1,0},{2,3},{3,2},{4,5},{5,4},{6,7},{7,6},{8,9},{9,8},{10,11... | collective-permute-start | bytes 1572872 | tf_op jit(solution)/shard_map/ppermute | solution.py:29
  111.0 7.4 %collective-permute-start.31 = (f32[4,64,512]{2,1,0:T(8,128)S(1)}, f32[4,64,512]{2,1,0:T(8,128)}, u32[]{:S(2)}, u32[]{:S(2)}) collective-permute-start(f32[4,64,512]{2,1,0:T(8,128)S(1)} %collective-permute-done.30.refs_4_), channel_id=1, source_target_pairs={{0,1},{1,0},{2,3},{3,2},{4,5},{5,4},{6,7},{7,6},{8,9},{9,8},{10,11... | collective-permute-start | bytes 1572872 | tf_op jit(solution)/shard_map/ppermute | solution.py:29
  111.1 14.6 %collective-permute-start.15 = (f32[4,64,512]{2,1,0:T(8,128)S(1)}, f32[4,64,512]{2,1,0:T(8,128)S(1)}, u32[]{:S(2)}, u32[]{:S(2)}) collective-permute-start(f32[4,64,512]{2,1,0:T(8,128)S(1)} %collective-permute-done.11.refs_8_), channel_id=1, source_target_pairs={{0,64},{1,65},{2,66},{3,67},{4,68},{5,69},{6,70},{7,71},{8,72},{9,... | collective-permute-start | bytes 1572872 | tf_op jit(solution)/shard_map/ppermute | solution.py:29
  113.9 14.5 %collective-permute-start.12 = (f32[4,64,512]{2,1,0:T(8,128)S(1)}, f32[4,64,512]{2,1,0:T(8,128)S(1)}, u32[]{:S(2)}, u32[]{:S(2)}) collective-permute-start(f32[4,64,512]{2,1,0:T(8,128)S(1)} %collective-permute-done.11.refs_8_), channel_id=1, source_target_pairs={{0,16},{1,17},{2,18},{3,19},{4,20},{5,21},{6,22},{7,23},{8,24},{9,... | collective-permute-start | bytes 1572872 | tf_op jit(solution)/shard_map/ppermute | solution.py:29
  114.5 14.1 %collective-permute-start.13 = (f32[4,64,512]{2,1,0:T(8,128)S(1)}, f32[4,64,512]{2,1,0:T(8,128)S(1)}, u32[]{:S(2)}, u32[]{:S(2)}) collective-permute-start(f32[4,64,512]{2,1,0:T(8,128)S(1)} %collective-permute-done.11.refs_8_), channel_id=1, source_target_pairs={{0,48},{1,49},{2,50},{3,51},{4,52},{5,53},{6,54},{7,55},{8,56},{9,... | collective-permute-start | bytes 1572872 | tf_op jit(solution)/shard_map/ppermute | solution.py:29
  117.6 22.3 %collective-permute-start.41 = (f32[4,64,512]{2,1,0:T(8,128)}, f32[4,64,512]{2,1,0:T(8,128)}, u32[]{:S(2)}, u32[]{:S(2)}) collective-permute-start(f32[4,64,512]{2,1,0:T(8,128)} %collective-permute-done.39.refs_12_), channel_id=1, source_target_pairs={{0,48},{1,49},{2,50},{3,51},{4,52},{5,53},{6,54},{7,55},{8,56},{9,... | collective-permute-start | bytes 1572872 | tf_op jit(solution)/shard_map/ppermute | solution.py:29
  118.4 25.6 %collective-permute-start.23 = (f32[4,64,512]{2,1,0:T(8,128)S(1)}, f32[4,64,512]{2,1,0:T(8,128)}, u32[]{:S(2)}, u32[]{:S(2)}) collective-permute-start(f32[4,64,512]{2,1,0:T(8,128)S(1)} %collective-permute-done.22.refs_6_), channel_id=1, source_target_pairs={{0,1},{1,0},{2,3},{3,2},{4,5},{5,4},{6,7},{7,6},{8,9},{9,8},{10,11... | collective-permute-start | bytes 1572872 | tf_op jit(solution)/shard_map/ppermute | solution.py:29
  125.7 51.4 %copy-start.1 = (f32[4,64,512]{2,1,0:T(8,128)}, f32[4,64,512]{2,1,0:T(8,128)S(1)}, u32[]{:S(2)}) copy-start(f32[4,64,512]{2,1,0:T(8,128)S(1)} %collective-permute-done.15.refs_12_) | copy-start | bytes 1572868
  125.7 19.5 %collective-permute-start.40 = (f32[4,64,512]{2,1,0:T(8,128)}, f32[4,64,512]{2,1,0:T(8,128)}, u32[]{:S(2)}, u32[]{:S(2)}) collective-permute-start(f32[4,64,512]{2,1,0:T(8,128)} %collective-permute-done.39.refs_12_), channel_id=1, source_target_pairs={{0,16},{1,17},{2,18},{3,19},{4,20},{5,21},{6,22},{7,23},{8,24},{9,... | collective-permute-start | bytes 1572872 | tf_op jit(solution)/shard_map/ppermute | solution.py:29
  128.4 48.7 %copy-start.2 = (f32[4,64,512]{2,1,0:T(8,128)}, f32[4,64,512]{2,1,0:T(8,128)S(1)}, u32[]{:S(2)}) copy-start(f32[4,64,512]{2,1,0:T(8,128)S(1)} %collective-permute-done.12.refs_9_) | copy-start | bytes 1572868
  128.4 22.3 %collective-permute-start.38 = (f32[4,64,512]{2,1,0:T(8,128)}, f32[4,64,512]{2,1,0:T(8,128)}, u32[]{:S(2)}, u32[]{:S(2)}) collective-permute-start(f32[4,64,512]{2,1,0:T(8,128)} %copy-done.20), channel_id=1, source_target_pairs={{0,16},{1,17},{2,18},{3,19},{4,20},{5,21},{6,22},{7,23},{8,24},{9,... | collective-permute-start | bytes 1572872 | tf_op jit(solution)/shard_map/ppermute | solution.py:29
  128.6 48.6 %copy-start.3 = (f32[4,64,512]{2,1,0:T(8,128)}, f32[4,64,512]{2,1,0:T(8,128)S(1)}, u32[]{:S(2)}) copy-start(f32[4,64,512]{2,1,0:T(8,128)S(1)} %collective-permute-done.13.refs_10_) | copy-start | bytes 1572868
  128.6 26.0 %collective-permute-start.17 = (f32[4,64,512]{2,1,0:T(8,128)S(1)}, f32[4,64,512]{2,1,0:T(8,128)S(1)}, u32[]{:S(2)}, u32[]{:S(2)}) collective-permute-start(f32[4,64,512]{2,1,0:T(8,128)S(1)} %collective-permute-done.15.refs_12_), channel_id=1, source_target_pairs={{0,48},{1,49},{2,50},{3,51},{4,52},{5,53},{6,54},{7,55},{8,56},{9,... | collective-permute-start | bytes 1572872 | tf_op jit(solution)/shard_map/ppermute | solution.py:29
  139.9 22.5 %collective-permute-start.42 = (f32[4,64,512]{2,1,0:T(8,128)}, f32[4,64,512]{2,1,0:T(8,128)}, u32[]{:S(2)}, u32[]{:S(2)}) collective-permute-start(f32[4,64,512]{2,1,0:T(8,128)} %collective-permute-done.41.refs_14_), channel_id=1, source_target_pairs={{0,48},{1,49},{2,50},{3,51},{4,52},{5,53},{6,54},{7,55},{8,56},{9,... | collective-permute-start | bytes 1572872 | tf_op jit(solution)/shard_map/ppermute | solution.py:29
  144.0 33.2 %collective-permute-start.8 = (f32[4,64,512]{2,1,0:T(8,128)}, f32[4,64,512]{2,1,0:T(8,128)}, u32[]{:S(2)}, u32[]{:S(2)}) collective-permute-start(f32[4,64,512]{2,1,0:T(8,128)} %copy-done.15), channel_id=1, source_target_pairs={{0,12},{1,13},{2,14},{3,15},{4,0},{5,1},{6,2},{7,3},{8,4},{9,5},{1... | collective-permute-start | bytes 1572872 | tf_op jit(solution)/shard_map/ppermute | solution.py:29
  145.2 33.5 %collective-permute-start.16 = (f32[4,64,512]{2,1,0:T(8,128)S(1)}, f32[4,64,512]{2,1,0:T(8,128)S(1)}, u32[]{:S(2)}, u32[]{:S(2)}) collective-permute-start(f32[4,64,512]{2,1,0:T(8,128)S(1)} %collective-permute-done.15.refs_12_), channel_id=1, source_target_pairs={{0,16},{1,17},{2,18},{3,19},{4,20},{5,21},{6,22},{7,23},{8,24},{9,... | collective-permute-start | bytes 1572872 | tf_op jit(solution)/shard_map/ppermute | solution.py:29
  150.7 28.0 %collective-permute-start.33 = (f32[4,64,512]{2,1,0:T(8,128)}, f32[4,64,512]{2,1,0:T(8,128)}, u32[]{:S(2)}, u32[]{:S(2)}) collective-permute-start(f32[4,64,512]{2,1,0:T(8,128)} %copy-done.22), channel_id=1, source_target_pairs={{0,1},{1,0},{2,3},{3,2},{4,5},{5,4},{6,7},{7,6},{8,9},{9,8},{10,11... | collective-permute-start | bytes 1572872 | tf_op jit(solution)/shard_map/ppermute | solution.py:29
  154.6 24.6 %collective-permute-start.14 = (f32[4,64,512]{2,1,0:T(8,128)S(1)}, f32[4,64,512]{2,1,0:T(8,128)}, u32[]{:S(2)}, u32[]{:S(2)}) collective-permute-start(f32[4,64,512]{2,1,0:T(8,128)S(1)} %collective-permute-done.12.refs_9_), channel_id=1, source_target_pairs={{0,16},{1,17},{2,18},{3,19},{4,20},{5,21},{6,22},{7,23},{8,24},{9,... | collective-permute-start | bytes 1572872 | tf_op jit(solution)/shard_map/ppermute | solution.py:29
  162.4 28.4 %collective-permute-start.18 = (f32[4,64,512]{2,1,0:T(8,128)S(1)}, f32[4,64,512]{2,1,0:T(8,128)}, u32[]{:S(2)}, u32[]{:S(2)}) collective-permute-start(f32[4,64,512]{2,1,0:T(8,128)S(1)} %collective-permute-done.17.refs_14_), channel_id=1, source_target_pairs={{0,48},{1,49},{2,50},{3,51},{4,52},{5,53},{6,54},{7,55},{8,56},{9,... | collective-permute-start | bytes 1572872 | tf_op jit(solution)/shard_map/ppermute | solution.py:29
  177.1 25.4 %collective-permute-start.1 = (f32[4,64,512]{2,1,0:T(8,128)}, f32[4,64,512]{2,1,0:T(8,128)S(1)}, u32[]{:S(2)}, u32[]{:S(2)}) collective-permute-start(f32[4,64,512]{2,1,0:T(8,128)} %copy-done.7), channel_id=1, source_target_pairs={{0,1},{1,0},{2,3},{3,2},{4,5},{5,4},{6,7},{7,6},{8,9},{9,8},{10,11... | collective-permute-start | bytes 1572872 | tf_op jit(solution)/shard_map/ppermute | solution.py:29
  178.6 23.9 %collective-permute-start.4 = (f32[4,64,512]{2,1,0:T(8,128)}, f32[4,64,512]{2,1,0:T(8,128)S(1)}, u32[]{:S(2)}, u32[]{:S(2)}) collective-permute-start(f32[4,64,512]{2,1,0:T(8,128)} %copy-done.15), channel_id=1, source_target_pairs={{0,1},{1,0},{2,3},{3,2},{4,5},{5,4},{6,7},{7,6},{8,9},{9,8},{10,11... | collective-permute-start | bytes 1572872 | tf_op jit(solution)/shard_map/ppermute | solution.py:29
  178.8 23.9 %collective-permute-start.7 = (f32[4,64,512]{2,1,0:T(8,128)}, f32[4,64,512]{2,1,0:T(8,128)S(1)}, u32[]{:S(2)}, u32[]{:S(2)}) collective-permute-start(f32[4,64,512]{2,1,0:T(8,128)} %copy-done.18), channel_id=1, source_target_pairs={{0,1},{1,0},{2,3},{3,2},{4,5},{5,4},{6,7},{7,6},{8,9},{9,8},{10,11... | collective-permute-start | bytes 1572872 | tf_op jit(solution)/shard_map/ppermute | solution.py:29
  179.2 23.5 %collective-permute-start.9 = (f32[4,64,512]{2,1,0:T(8,128)}, f32[4,64,512]{2,1,0:T(8,128)S(1)}, u32[]{:S(2)}, u32[]{:S(2)}) collective-permute-start(f32[4,64,512]{2,1,0:T(8,128)} %collective-permute-done.8.refs_6_), channel_id=1, source_target_pairs={{0,1},{1,0},{2,3},{3,2},{4,5},{5,4},{6,7},{7,6},{8,9},{9,8},{10,11... | collective-permute-start | bytes 1572872 | tf_op jit(solution)/shard_map/ppermute | solution.py:29
  (20 other events, 220.5 us)

commit v2 on v1

--- a/solution.py
+++ b/solution.py
@@ -66,7 +66,7 @@
 
 
 OFFSETS = (0, 3, 1, 2)
-CALLS = (((0, 2), (2, 4)), ((0, 2), (2, 4)))
+CALLS = (((0, 2), (2, 4)), ((0, 4),))
 
 
 def split(value):
@@ -75,7 +75,17 @@
     return high, low
 
 
-def density_kernel(add, tiles, tile_ref, within_ref, slot_ref, *refs):
+def density_kernel(add, first, tiles, *refs):
+    row, col = lax.axis_index("row"), lax.axis_index("col")
+    x, pair = lax.div(col, 4), lax.rem(col, 4)
+    y_hi, z = lax.div(row, 4), lax.rem(row, 4)
+    source = lax.rem(x, 2) * 2 + lax.div(pair, 2)
+
+    def slot_of(n):
+        turn = lax.rem(z + OFFSETS[n % 4] + 4 - source, 4)
+        base = lax.rem(turn, 2) * 2 + lax.div(turn, 2)
+        return (y_hi if n < 4 else 1 - y_hi) * 4 + base
+
     rows, columns, refs = refs[: 4 * tiles], refs[4 * tiles : 4 * tiles + 8], refs[4 * tiles + 8 :]
     if add is not None:
         before, refs = refs[0], refs[1:]
@@ -85,7 +95,9 @@
     count, last = 4 * height, mats - 1
 
     def block(ref, t):
-        start = pl.multiple_of(tile_ref[t] * count, count)
+        t = t + first
+        offset = jnp.where(t == 0, 0, jnp.where(t == 1, 3, t - 1))
+        start = pl.multiple_of(lax.rem(x + offset, 4) * count, count)
         return ref.at[:, pl.ds(start, count), :]
 
     def fetch_rows(i, source):
@@ -109,7 +121,7 @@
             fetch_held(t).start()
     for n, copy in enumerate(copies):
         copy.wait()
-        slot = slot_ref[n]
+        slot = slot_of(n)
         high, low = split(col_full[n])
         col_high[:, slot] = high
         col_low[:, slot] = low
@@ -124,8 +136,8 @@
             i = 4 * t + n
             fetch_rows(i, rows[n]).wait()
             high, low = split(row_full[i])
-            row_high[:, n ^ within_ref[0]] = high
-            row_low[:, n ^ within_ref[0]] = low
+            row_high[:, n ^ pair] = high
+            row_low[:, n ^ pair] = low
         if add:
             fetch_held(t).wait()
 
@@ -153,7 +165,7 @@
         store(t).wait()
 
 
-def add_tiles(rows, columns, where, within, slots, before, add):
+def add_tiles(rows, columns, first, before, add):
     tiles = len(rows) // 4
     mats, height, depth = rows[0].shape
     count, width = 4 * height, 8 * height
@@ -164,10 +176,10 @@
         operands.append(before)
     vmem = lambda shape, dtype: pltpu.VMEM(shape, dtype)
     return pl.pallas_call(
-        functools.partial(density_kernel, add, tiles),
+        functools.partial(density_kernel, add, first, tiles),
         out_shape=jax.ShapeDtypeStruct((mats - 1, 4 * count, width), jnp.float32),
         grid_spec=pltpu.PrefetchScalarGridSpec(
-            num_scalar_prefetch=3,
+            num_scalar_prefetch=0,
             grid=(1,),
             in_specs=[pl.BlockSpec(memory_space=pltpu.HBM)] * len(operands),
             out_specs=pl.BlockSpec(memory_space=pltpu.HBM),
@@ -186,41 +198,30 @@
                 pltpu.SemaphoreType.DMA((2,)),
             ],
         ),
-        input_output_aliases={} if before is None else {2 + len(operands): 0},
+        input_output_aliases={} if before is None else {len(operands) - 1: 0},
         cost_estimate=pl.CostEstimate(
             flops=2 * 6 * (mats - 1) * tiles * count * width * depth,
             bytes_accessed=(len(rows) + 8) * mats * height * depth * 4,
             transcendentals=0,
         ),
-    )(where, within, slots, *operands)
+    )(*operands)
 
 
 def whole(response_coeffs, occupied_coeffs):
-    own = jnp.concatenate([response_coeffs, occupied_coeffs[None]], axis=0)
-    row, col = lax.axis_index("row"), lax.axis_index("col")
-    x, pair = col // 4, col % 4
-    y_hi, z = row // 4, row % 4
-    source = (x % 2) * 2 + pair // 2
-    parts = [own[:, :, s : s + d] for s, d in PIECES]
+    parts = [
+        jnp.concatenate(
+            [response_coeffs[:, :, s : s + d], occupied_coeffs[None, :, s : s + d]]
+        )
+        for s, d in PIECES
+    ]
     columns = [gather_columns(part) for part in parts]
     tiles = [gather_rows(part) for part in parts]
-    turn = (z + jnp.array(OFFSETS) - source) % 4
-    base = turn % 2 * 2 + turn // 2
-    slots = jnp.concatenate([y_hi * 4 + base, (1 - y_hi) * 4 + base]).astype(jnp.int32)
-    where = ((x + jnp.array(OFFSETS)) % 4).astype(jnp.int32)
-    within = pair[None].astype(jnp.int32)
     density = None
     for n, (entry, other) in enumerate(columns):
         for start, stop in CALLS[n]:
             rows = sum(tiles[n][2 * start : 2 * stop], ())
             density = add_tiles(
-                rows,
-                (*entry, *other),
-                where[start:stop],
-                within,
-                slots,
-                density,
-                n > 0,
+                rows, (*entry, *other), start, density, n > 0
             )
     return density
 

time: 218 us -> 218 us (level)
  the two profiles are of different devices: /device:TPU:1 before, /device:TPU:8 now
where the time goes in v2:
time: 218 us
  waiting for transfers between devices  94.4 us (43%)
  starting transfers between devices  78.3 us (36%)
  Pallas kernels  40.2 us (18%)
  local copies, waits for them, and re-layouts  4.02 us (2%)
    ppermute x48, waiting for transfers between devices, move(): return lax.ppermute(value, AXES, pairs)  94.4 us
    ppermute x48, starting transfers between devices, move(): return lax.ppermute(value, AXES, pairs)  78.3 us
    pallas_call x3, Pallas kernels, add_tiles(): pl.pallas_call(functools.partial(density_kernel, add, first, tiles), out_...  40.2 us
  transfers between devices with their start and end apart: 48, of which 20 were waited for; matrix products, arithmetic and copies ran while one was open for 0% of the time, Pallas kernels for 10%

profile of v2, /device:TPU:8, one launch (start us, length us, event | category | flops | bytes accessed | tf_op | source)
XLA Modules:
  0.0 217.7 jit_solution(17262031565134806693)
XLA Ops:
  0.0 1.2 fusion
  1.2 1.0 slice_bitcast_fusion
  2.2 3.8 %collective-permute-start.34 = (f32[4,64,512]{2,1,0:T(8,128)S(1)}, f32[4,64,512]{2,1,0:T(8,128)S(1)}, u32[]{:S(2)}, u32[]{:S(2)}) collective-permute-start(f32[4,64,512]{2,1,0:T(8,128)S(1)} %pad_maximum_fusion.1.refs_0_), channel_id=1, source_target_pairs={{0,0},{1,33},{2,18},{3,51},{4,4},{5,37},{6,22},{7,55},{8,8},{9,41}... | collective-permute-start | bytes 1572872 | tf_op jit(solution)/shard_map/ppermute | solution.py:29
  6.0 0.1 collective-permute-start.26
  6.1 1.6 collective-permute-start.29
  7.7 1.4 collective-permute-start.43
  9.1 1.7 collective-permute-start.24
  10.9 4.4 %collective-permute-done.34 = f32[4,64,512]{2,1,0:T(8,128)S(1)} collective-permute-done((f32[4,64,512]{2,1,0:T(8,128)S(1)}, f32[4,64,512]{2,1,0:T(8,128)S(1)}, u32[]{:S(2)}, u32[]{:S(2)}) %collective-permute-start.34) | collective-permute-done | bytes 524320 | tf_op jit(solution)/shard_map/ppermute | solution.py:29
  15.3 1.9 collective-permute-start.15
  17.2 3.0 %collective-permute-done.26.refs_2_ = f32[4,64,512]{2,1,0:T(8,128)S(1)} collective-permute-done((f32[4,64,512]{2,1,0:T(8,128)S(1)}, f32[4,64,512]{2,1,0:T(8,128)S(1)}, u32[]{:S(2)}, u32[]{:S(2)}) %collective-permute-start.26) | collective-permute-done | bytes 524320 | tf_op jit(solution)/shard_map/ppermute | solution.py:29
  20.2 1.3 collective-permute-done.29.refs_4_
  21.5 0.3 collective-permute-start.3
  21.8 3.0 %collective-permute-start.7 = (f32[4,64,512]{2,1,0:T(8,128)S(1)}, f32[4,64,512]{2,1,0:T(8,128)S(1)}, u32[]{:S(2)}, u32[]{:S(2)}) collective-permute-start(f32[4,64,512]{2,1,0:T(8,128)S(1)} %pad_maximum_fusion.refs_0_), channel_id=1, source_target_pairs={{0,12},{1,13},{2,14},{3,15},{4,0},{5,1},{6,2},{7,3},{8,4},{9,5},{1... | collective-permute-start | bytes 1572872 | tf_op jit(solution)/shard_map/ppermute | solution.py:29
  24.8 0.3 collective-permute-start
  25.0 2.6 %collective-permute-done.15 = f32[4,64,512]{2,1,0:T(8,128)S(1)} collective-permute-done((f32[4,64,512]{2,1,0:T(8,128)S(1)}, f32[4,64,512]{2,1,0:T(8,128)S(1)}, u32[]{:S(2)}, u32[]{:S(2)}) %collective-permute-start.15) | collective-permute-done | bytes 524320 | tf_op jit(solution)/shard_map/ppermute | solution.py:29
  27.6 3.4 %collective-permute-start.35 = (f32[4,64,512]{2,1,0:T(8,128)S(1)}, f32[4,64,512]{2,1,0:T(8,128)S(1)}, u32[]{:S(2)}, u32[]{:S(2)}) collective-permute-start(f32[4,64,512]{2,1,0:T(8,128)S(1)} %collective-permute-done.34), channel_id=1, source_target_pairs={{0,0},{1,4},{2,6},{3,2},{4,64},{5,68},{6,70},{7,66},{8,1},{9,5},{1... | collective-permute-start | bytes 1572872 | tf_op jit(solution)/shard_map/ppermute | solution.py:29
  31.0 3.9 %collective-permute-done.1.refs_2_ = f32[4,64,512]{2,1,0:T(8,128)S(1)} collective-permute-done((f32[4,64,512]{2,1,0:T(8,128)S(1)}, f32[4,64,512]{2,1,0:T(8,128)S(1)}, u32[]{:S(2)}, u32[]{:S(2)}) %collective-permute-start.1) | collective-permute-done | bytes 524320 | tf_op jit(solution)/shard_map/ppermute | solution.py:29
  34.9 1.6 collective-permute-start.46
  36.5 4.8 %collective-permute-done.3.refs_4_ = f32[4,64,512]{2,1,0:T(8,128)S(1)} collective-permute-done((f32[4,64,512]{2,1,0:T(8,128)S(1)}, f32[4,64,512]{2,1,0:T(8,128)S(1)}, u32[]{:S(2)}, u32[]{:S(2)}) %collective-permute-start.3) | collective-permute-done | bytes 524320 | tf_op jit(solution)/shard_map/ppermute | solution.py:29
  41.3 0.5 collective-permute-start.45
  41.8 0.9 collective-permute-done.35.refs_8_
  42.7 2.8 %collective-permute-start.30 = (f32[4,64,512]{2,1,0:T(8,128)S(1)}, f32[4,64,512]{2,1,0:T(8,128)S(1)}, u32[]{:S(2)}, u32[]{:S(2)}) collective-permute-start(f32[4,64,512]{2,1,0:T(8,128)S(1)} %collective-permute-done.29.refs_4_), channel_id=1, source_target_pairs={{0,4},{1,5},{2,6},{3,7},{4,8},{5,9},{6,10},{7,11},{8,12},{9,13},{1... | collective-permute-start | bytes 1572872 | tf_op jit(solution)/shard_map/ppermute | solution.py:29
  45.6 8.8 %collective-permute-done.46.refs_6_ = f32[4,64,512]{2,1,0:T(8,128)S(1)} collective-permute-done((f32[4,64,512]{2,1,0:T(8,128)S(1)}, f32[4,64,512]{2,1,0:T(8,128)S(1)}, u32[]{:S(2)}, u32[]{:S(2)}) %collective-permute-start.46) | collective-permute-done | bytes 524320 | tf_op jit(solution)/shard_map/ppermute | solution.py:29
  54.4 8.9 %collective-permute-start.25 = (f32[4,64,512]{2,1,0:T(8,128)S(1)}, f32[4,64,512]{2,1,0:T(8,128)S(1)}, u32[]{:S(2)}, u32[]{:S(2)}) collective-permute-start(f32[4,64,512]{2,1,0:T(8,128)S(1)} %collective-permute-done.24.refs_0_), channel_id=1, source_target_pairs={{0,1},{1,0},{2,3},{3,2},{4,5},{5,4},{6,7},{7,6},{8,9},{9,8},{10,11... | collective-permute-start | bytes 1572872 | tf_op jit(solution)/shard_map/ppermute | solution.py:29
  63.3 1.9 collective-permute-start.16
  65.2 1.1 collective-permute-start.9
  66.3 1.0 collective-permute-start.5
  67.3 0.5 collective-permute-done.30.refs_4_
  67.8 7.3 %collective-permute-start.2 = (f32[4,64,512]{2,1,0:T(8,128)S(1)}, f32[4,64,512]{2,1,0:T(8,128)S(1)}, u32[]{:S(2)}, u32[]{:S(2)}) collective-permute-start(f32[4,64,512]{2,1,0:T(8,128)S(1)} %collective-permute-done.1.refs_2_), channel_id=1, source_target_pairs={{0,1},{1,0},{2,3},{3,2},{4,5},{5,4},{6,7},{7,6},{8,9},{9,8},{10,11... | collective-permute-start | bytes 1572872 | tf_op jit(solution)/shard_map/ppermute | solution.py:29
  75.1 1.0 collective-permute-done.16.refs_16_
  76.1 4.2 %collective-permute-start.4 = (f32[4,64,512]{2,1,0:T(8,128)S(1)}, f32[4,64,512]{2,1,0:T(8,128)S(1)}, u32[]{:S(2)}, u32[]{:S(2)}) collective-permute-start(f32[4,64,512]{2,1,0:T(8,128)S(1)} %collective-permute-done.3.refs_4_), channel_id=1, source_target_pairs={{0,1},{1,0},{2,3},{3,2},{4,5},{5,4},{6,7},{7,6},{8,9},{9,8},{10,11... | collective-permute-start | bytes 1572872 | tf_op jit(solution)/shard_map/ppermute | solution.py:29
  80.3 0.1 collective-permute-start.8
  80.4 6.9 %collective-permute-done.5.refs_6_ = f32[4,64,512]{2,1,0:T(8,128)S(1)} collective-permute-done((f32[4,64,512]{2,1,0:T(8,128)S(1)}, f32[4,64,512]{2,1,0:T(8,128)S(1)}, u32[]{:S(2)}, u32[]{:S(2)}) %collective-permute-start.5) | collective-permute-done | bytes 524320 | tf_op jit(solution)/shard_map/ppermute | solution.py:29
  87.3 4.6 %collective-permute-start.39 = (f32[4,64,512]{2,1,0:T(8,128)S(1)}, f32[4,64,512]{2,1,0:T(8,128)S(1)}, u32[]{:S(2)}, u32[]{:S(2)}) collective-permute-start(f32[4,64,512]{2,1,0:T(8,128)S(1)} %collective-permute-done.35.refs_8_), channel_id=1, source_target_pairs={{0,64},{1,65},{2,66},{3,67},{4,68},{5,69},{6,70},{7,71},{8,72},{9,... | collective-permute-start | bytes 1572872 | tf_op jit(solution)/shard_map/ppermute | solution.py:29
  91.9 6.3 %collective-permute-done.11.refs_12_ = f32[4,64,512]{2,1,0:T(8,128)S(1)} collective-permute-done((f32[4,64,512]{2,1,0:T(8,128)S(1)}, f32[4,64,512]{2,1,0:T(8,128)S(1)}, u32[]{:S(2)}, u32[]{:S(2)}) %collective-permute-start.11) | collective-permute-done | bytes 524320 | tf_op jit(solution)/shard_map/ppermute | solution.py:29
  98.2 8.0 %collective-permute-start.36 = (f32[4,64,512]{2,1,0:T(8,128)S(1)}, f32[4,64,512]{2,1,0:T(8,128)S(1)}, u32[]{:S(2)}, u32[]{:S(2)}) collective-permute-start(f32[4,64,512]{2,1,0:T(8,128)S(1)} %collective-permute-done.35.refs_8_), channel_id=1, source_target_pairs={{0,16},{1,17},{2,18},{3,19},{4,20},{5,21},{6,22},{7,23},{8,24},{9,... | collective-permute-start | bytes 1572872 | tf_op jit(solution)/shard_map/ppermute | solution.py:29
  106.2 0.1 collective-permute-start.37
  106.3 1.4 collective-permute-start.47
  107.8 0.9 collective-permute-start.28
  108.7 7.8 %collective-permute-done.36.refs_9_ = f32[4,64,512]{2,1,0:T(8,128)S(1)} collective-permute-done((f32[4,64,512]{2,1,0:T(8,128)S(1)}, f32[4,64,512]{2,1,0:T(8,128)S(1)}, u32[]{:S(2)}, u32[]{:S(2)}) %collective-permute-start.36) | collective-permute-done | bytes 524320 | tf_op jit(solution)/shard_map/ppermute | solution.py:29
  116.5 2.3 %collective-permute-done.37.refs_10_ = f32[4,64,512]{2,1,0:T(8,128)S(1)} collective-permute-done((f32[4,64,512]{2,1,0:T(8,128)S(1)}, f32[4,64,512]{2,1,0:T(8,128)S(1)}, u32[]{:S(2)}, u32[]{:S(2)}) %collective-permute-start.37) | collective-permute-done | bytes 524320 | tf_op jit(solution)/shard_map/ppermute | solution.py:29
  118.9 0.1 collective-permute-start.13
  118.9 0.9 copy-done.34
  119.9 2.0 collective-permute-done.32.refs_6_
  121.8 1.4 collective-permute-start.17
  123.2 0.1 collective-permute-start.6
  123.4 10.9 %collective-permute-done.20.refs_20_ = f32[4,64,512]{2,1,0:T(8,128)} collective-permute-done((f32[4,64,512]{2,1,0:T(8,128)}, f32[4,64,512]{2,1,0:T(8,128)}, u32[]{:S(2)}, u32[]{:S(2)}) %collective-permute-start.20) | collective-permute-done | bytes 524320 | tf_op jit(solution)/shard_map/ppermute | solution.py:29
  134.3 3.5 %collective-permute-start.41 = (f32[4,64,512]{2,1,0:T(8,128)S(1)}, f32[4,64,512]{2,1,0:T(8,128)S(1)}, u32[]{:S(2)}, u32[]{:S(2)}) collective-permute-start(f32[4,64,512]{2,1,0:T(8,128)S(1)} %collective-permute-done.39.refs_12_), channel_id=1, source_target_pairs={{0,48},{1,49},{2,50},{3,51},{4,52},{5,53},{6,54},{7,55},{8,56},{9,... | collective-permute-start | bytes 1572872 | tf_op jit(solution)/shard_map/ppermute | solution.py:29
  137.8 0.3 collective-permute-start.40
  138.1 0.1 collective-permute-start.38
  138.2 0.2 collective-permute-start.33
  138.5 3.1 %collective-permute-start.22 = (f32[4,64,512]{2,1,0:T(8,128)}, f32[4,64,512]{2,1,0:T(8,128)}, u32[]{:S(2)}, u32[]{:S(2)}) collective-permute-start(f32[4,64,512]{2,1,0:T(8,128)} %collective-permute-done.20.refs_20_), channel_id=1, source_target_pairs={{0,48},{1,49},{2,50},{3,51},{4,52},{5,53},{6,54},{7,55},{8,56},{9,... | collective-permute-start | bytes 1572872 | tf_op jit(solution)/shard_map/ppermute | solution.py:29
  141.6 8.5 %collective-permute-done.41.refs_14_ = f32[4,64,512]{2,1,0:T(8,128)S(1)} collective-permute-done((f32[4,64,512]{2,1,0:T(8,128)S(1)}, f32[4,64,512]{2,1,0:T(8,128)S(1)}, u32[]{:S(2)}, u32[]{:S(2)}) %collective-permute-start.41) | collective-permute-done | bytes 524320 | tf_op jit(solution)/shard_map/ppermute | solution.py:29
  150.1 3.7 %collective-permute-start.42 = (f32[4,64,512]{2,1,0:T(8,128)S(1)}, f32[4,64,512]{2,1,0:T(8,128)S(1)}, u32[]{:S(2)}, u32[]{:S(2)}) collective-permute-start(f32[4,64,512]{2,1,0:T(8,128)S(1)} %collective-permute-done.41.refs_14_), channel_id=1, source_target_pairs={{0,48},{1,49},{2,50},{3,51},{4,52},{5,53},{6,54},{7,55},{8,56},{9,... | collective-permute-start | bytes 1572872 | tf_op jit(solution)/shard_map/ppermute | solution.py:29
  153.8 0.2 collective-permute-done.40.refs_13_
  154.1 10.4 %collective-permute-done.38.refs_11_ = f32[4,64,512]{2,1,0:T(8,128)S(1)} collective-permute-done((f32[4,64,512]{2,1,0:T(8,128)S(1)}, f32[4,64,512]{2,1,0:T(8,128)S(1)}, u32[]{:S(2)}, u32[]{:S(2)}) %collective-permute-start.38) | collective-permute-done | bytes 524320 | tf_op jit(solution)/shard_map/ppermute | solution.py:29
  164.6 0.1 collective-permute-start.14
  164.7 0.1 collective-permute-start.19
  164.8 7.8 %collective-permute-done.42.refs_15_ = f32[4,64,512]{2,1,0:T(8,128)S(1)} collective-permute-done((f32[4,64,512]{2,1,0:T(8,128)S(1)}, f32[4,64,512]{2,1,0:T(8,128)S(1)}, u32[]{:S(2)}, u32[]{:S(2)}) %collective-permute-start.42) | collective-permute-done | bytes 524320 | tf_op jit(solution)/shard_map/ppermute | solution.py:29
  172.7 0.8 copy-done.15
  173.5 3.7 %collective-permute-start.23 = (f32[4,64,512]{2,1,0:T(8,128)}, f32[4,64,512]{2,1,0:T(8,128)}, u32[]{:S(2)}, u32[]{:S(2)}) collective-permute-start(f32[4,64,512]{2,1,0:T(8,128)} %collective-permute-done.22.refs_22_), channel_id=1, source_target_pairs={{0,48},{1,49},{2,50},{3,51},{4,52},{5,53},{6,54},{7,55},{8,56},{9,... | collective-permute-start | bytes 1572872 | tf_op jit(solution)/shard_map/ppermute | solution.py:29
  177.2 10.6 %shard_map.28.refs_16_ = f32[3,1024,512]{2,1,0:T(8,128)} custom-call(f32[4,64,512]{2,1,0:T(8,128)} %copy-done.17, f32[4,64,512]{2,1,0:T(8,128)} %copy-done.23, f32[4,64,512]{2,1,0:T(8,128)} %copy-done.20, f32[4,64,512]{2,1,0:T(8,128)} %copy-done.26, f32[4,64,512]{2,1,0:T(8,128)} %copy-done.22, f32[4,64,512]{2,1,0:T(8,128)} %collective-permute-done.45.refs_5_, ...), custom_call_target="tpu_custom_call" | custom-call | flops 4831838208 | bytes 8388608 | tf_op jit(solution)/shard_map/pallas_call | solution.py:178
  187.8 10.6 %shard_map.29.refs_24_ = f32[3,1024,512]{2,1,0:T(8,128)} custom-call(f32[4,64,512]{2,1,0:T(8,128)} %copy-done, f32[4,64,512]{2,1,0:T(8,128)} %copy-done.4, f32[4,64,512]{2,1,0:T(8,128)} %copy-done.2, f32[4,64,512]{2,1,0:T(8,128)} %copy-done.9, f32[4,64,512]{2,1,0:T(8,128)} %copy-done.3, f32[4,64,512]{2,1,0:T(8,128)} %copy-done.10, ...), custom_call_target="tpu_custom_call", output_to_operand_aliasing={{}: (16, {})} | custom-call | flops 4831838208 | bytes 8388608 | tf_op jit(solution)/shard_map/pallas_call | solution.py:178
  198.4 19.1 %shard_map.30 = f32[3,1024,512]{2,1,0:T(8,128)} custom-call(f32[4,64,512]{2,1,0:T(8,128)} %copy-done.16, f32[4,64,512]{2,1,0:T(8,128)} %copy-done.24, f32[4,64,512]{2,1,0:T(8,128)} %copy-done.18, f32[4,64,512]{2,1,0:T(8,128)} %copy-done.30, f32[4,64,512]{2,1,0:T(8,128)} %copy-done.19, f32[4,64,512]{2,1,0:T(8,128)} %copy-done.31, ...), custom_call_target="tpu_custom_call", output_to_operand_aliasing={{}: (24, {})} | custom-call | flops 9663676416 | bytes 12582912 | tf_op jit(solution)/shard_map/pallas_call | solution.py:178
  (113 shorter events, 0.4 us)
Async XLA Ops:
  2.2 170.4 %copy-start.17 = (f32[4,64,512]{2,1,0:T(8,128)}, f32[4,64,512]{2,1,0:T(8,128)S(1)}, u32[]{:S(2)}) copy-start(f32[4,64,512]{2,1,0:T(8,128)S(1)} %pad_maximum_fusion.1.refs_0_) | copy-start | bytes 1572868
  2.2 13.1 %collective-permute-start.34 = (f32[4,64,512]{2,1,0:T(8,128)S(1)}, f32[4,64,512]{2,1,0:T(8,128)S(1)}, u32[]{:S(2)}, u32[]{:S(2)}) collective-permute-start(f32[4,64,512]{2,1,0:T(8,128)S(1)} %pad_maximum_fusion.1.refs_0_), channel_id=1, source_target_pairs={{0,0},{1,33},{2,18},{3,51},{4,4},{5,37},{6,22},{7,55},{8,8},{9,41}... | collective-permute-start | bytes 1572872 | tf_op jit(solution)/shard_map/ppermute | solution.py:29
  6.0 14.2 %collective-permute-start.26 = (f32[4,64,512]{2,1,0:T(8,128)S(1)}, f32[4,64,512]{2,1,0:T(8,128)S(1)}, u32[]{:S(2)}, u32[]{:S(2)}) collective-permute-start(f32[4,64,512]{2,1,0:T(8,128)S(1)} %pad_maximum_fusion.1.refs_0_), channel_id=1, source_target_pairs={{0,2},{1,3},{2,0},{3,1},{4,6},{5,7},{6,4},{7,5},{8,10},{9,11},{10,... | collective-permute-start | bytes 1572872 | tf_op jit(solution)/shard_map/ppermute | solution.py:29
  6.1 15.4 %collective-permute-start.29 = (f32[4,64,512]{2,1,0:T(8,128)S(1)}, f32[4,64,512]{2,1,0:T(8,128)S(1)}, u32[]{:S(2)}, u32[]{:S(2)}) collective-permute-start(f32[4,64,512]{2,1,0:T(8,128)S(1)} %pad_maximum_fusion.1.refs_0_), channel_id=1, source_target_pairs={{0,4},{1,5},{2,6},{3,7},{4,8},{5,9},{6,10},{7,11},{8,12},{9,13},{1... | collective-permute-start | bytes 1572872 | tf_op jit(solution)/shard_map/ppermute | solution.py:29
  7.7 14.1 %collective-permute-start.43 = (f32[4,64,512]{2,1,0:T(8,128)S(1)}, f32[4,64,512]{2,1,0:T(8,128)S(1)}, u32[]{:S(2)}, u32[]{:S(2)}) collective-permute-start(f32[4,64,512]{2,1,0:T(8,128)S(1)} %pad_maximum_fusion.1.refs_0_), channel_id=1, source_target_pairs={{0,1},{1,0},{2,3},{3,2},{4,5},{5,4},{6,7},{7,6},{8,9},{9,8},{10,11... | collective-permute-start | bytes 1572872 | tf_op jit(solution)/shard_map/ppermute | solution.py:29
  9.1 15.7 %collective-permute-start.24 = (f32[4,64,512]{2,1,0:T(8,128)S(1)}, f32[4,64,512]{2,1,0:T(8,128)S(1)}, u32[]{:S(2)}, u32[]{:S(2)}) collective-permute-start(f32[4,64,512]{2,1,0:T(8,128)S(1)} %pad_maximum_fusion.1.refs_0_), channel_id=1, source_target_pairs={{0,12},{1,13},{2,14},{3,15},{4,0},{5,1},{6,2},{7,3},{8,4},{9,5},{1... | collective-permute-start | bytes 1572872 | tf_op jit(solution)/shard_map/ppermute | solution.py:29
  10.9 161.7 %copy-start.16 = (f32[4,64,512]{2,1,0:T(8,128)}, f32[4,64,512]{2,1,0:T(8,128)S(1)}, u32[]{:S(2)}) copy-start(f32[4,64,512]{2,1,0:T(8,128)S(1)} %pad_maximum_fusion.refs_0_) | copy-start | bytes 1572868
  15.3 12.3 %collective-permute-start.15 = (f32[4,64,512]{2,1,0:T(8,128)S(1)}, f32[4,64,512]{2,1,0:T(8,128)S(1)}, u32[]{:S(2)}, u32[]{:S(2)}) collective-permute-start(f32[4,64,512]{2,1,0:T(8,128)S(1)} %pad_maximum_fusion.refs_0_), channel_id=1, source_target_pairs={{0,0},{1,33},{2,18},{3,51},{4,4},{5,37},{6,22},{7,55},{8,8},{9,41}... | collective-permute-start | bytes 1572872 | tf_op jit(solution)/shard_map/ppermute | solution.py:29
  20.2 152.4 %copy-start.20 = (f32[4,64,512]{2,1,0:T(8,128)}, f32[4,64,512]{2,1,0:T(8,128)S(1)}, u32[]{:S(2)}) copy-start(f32[4,64,512]{2,1,0:T(8,128)S(1)} %collective-permute-done.26.refs_2_) | copy-start | bytes 1572868
  20.2 14.7 %collective-permute-start.1 = (f32[4,64,512]{2,1,0:T(8,128)S(1)}, f32[4,64,512]{2,1,0:T(8,128)S(1)}, u32[]{:S(2)}, u32[]{:S(2)}) collective-permute-start(f32[4,64,512]{2,1,0:T(8,128)S(1)} %pad_maximum_fusion.refs_0_), channel_id=1, source_target_pairs={{0,2},{1,3},{2,0},{3,1},{4,6},{5,7},{6,4},{7,5},{8,10},{9,11},{10,... | collective-permute-start | bytes 1572872 | tf_op jit(solution)/shard_map/ppermute | solution.py:29
  21.5 151.1 %copy-start.22 = (f32[4,64,512]{2,1,0:T(8,128)}, f32[4,64,512]{2,1,0:T(8,128)S(1)}, u32[]{:S(2)}) copy-start(f32[4,64,512]{2,1,0:T(8,128)S(1)} %collective-permute-done.29.refs_4_) | copy-start | bytes 1572868
  21.5 19.8 %collective-permute-start.3 = (f32[4,64,512]{2,1,0:T(8,128)S(1)}, f32[4,64,512]{2,1,0:T(8,128)S(1)}, u32[]{:S(2)}, u32[]{:S(2)}) collective-permute-start(f32[4,64,512]{2,1,0:T(8,128)S(1)} %pad_maximum_fusion.refs_0_), channel_id=1, source_target_pairs={{0,4},{1,5},{2,6},{3,7},{4,8},{5,9},{6,10},{7,11},{8,12},{9,13},{1... | collective-permute-start | bytes 1572872 | tf_op jit(solution)/shard_map/ppermute | solution.py:29
  21.8 150.8 %copy-start.23 = (f32[4,64,512]{2,1,0:T(8,128)}, f32[4,64,512]{2,1,0:T(8,128)S(1)}, u32[]{:S(2)}) copy-start(f32[4,64,512]{2,1,0:T(8,128)S(1)} %collective-permute-done.43.refs_1_) | copy-start | bytes 1572868
  21.8 19.5 %collective-permute-start.7 = (f32[4,64,512]{2,1,0:T(8,128)S(1)}, f32[4,64,512]{2,1,0:T(8,128)S(1)}, u32[]{:S(2)}, u32[]{:S(2)}) collective-permute-start(f32[4,64,512]{2,1,0:T(8,128)S(1)} %pad_maximum_fusion.refs_0_), channel_id=1, source_target_pairs={{0,12},{1,13},{2,14},{3,15},{4,0},{5,1},{6,2},{7,3},{8,4},{9,5},{1... | collective-permute-start | bytes 1572872 | tf_op jit(solution)/shard_map/ppermute | solution.py:29
  24.8 163.0 %copy-start = (f32[4,64,512]{2,1,0:T(8,128)}, f32[4,64,512]{2,1,0:T(8,128)S(1)}, u32[]{:S(2)}) copy-start(f32[4,64,512]{2,1,0:T(8,128)S(1)} %collective-permute-done.24.refs_0_) | copy-start | bytes 1572868
  24.8 17.0 %collective-permute-start = (f32[4,64,512]{2,1,0:T(8,128)S(1)}, f32[4,64,512]{2,1,0:T(8,128)S(1)}, u32[]{:S(2)}, u32[]{:S(2)}) collective-permute-start(f32[4,64,512]{2,1,0:T(8,128)S(1)} %pad_maximum_fusion.refs_0_), channel_id=1, source_target_pairs={{0,1},{1,0},{2,3},{3,2},{4,5},{5,4},{6,7},{7,6},{8,9},{9,8},{10,11... | collective-permute-start | bytes 1572872 | tf_op jit(solution)/shard_map/ppermute | solution.py:29
  27.6 15.1 %collective-permute-start.35 = (f32[4,64,512]{2,1,0:T(8,128)S(1)}, f32[4,64,512]{2,1,0:T(8,128)S(1)}, u32[]{:S(2)}, u32[]{:S(2)}) collective-permute-start(f32[4,64,512]{2,1,0:T(8,128)S(1)} %collective-permute-done.34), channel_id=1, source_target_pairs={{0,0},{1,4},{2,6},{3,2},{4,64},{5,68},{6,70},{7,66},{8,1},{9,5},{1... | collective-permute-start | bytes 1572872 | tf_op jit(solution)/shard_map/ppermute | solution.py:29
  34.9 71.3 %copy-start.18 = (f32[4,64,512]{2,1,0:T(8,128)}, f32[4,64,512]{2,1,0:T(8,128)S(1)}, u32[]{:S(2)}) copy-start(f32[4,64,512]{2,1,0:T(8,128)S(1)} %collective-permute-done.1.refs_2_) | copy-start | bytes 1572868
  34.9 19.5 %collective-permute-start.46 = (f32[4,64,512]{2,1,0:T(8,128)S(1)}, f32[4,64,512]{2,1,0:T(8,128)S(1)}, u32[]{:S(2)}, u32[]{:S(2)}) collective-permute-start(f32[4,64,512]{2,1,0:T(8,128)S(1)} %collective-permute-done.26.refs_2_), channel_id=1, source_target_pairs={{0,4},{1,5},{2,6},{3,7},{4,8},{5,9},{6,10},{7,11},{8,12},{9,13},{1... | collective-permute-start | bytes 1572872 | tf_op jit(solution)/shard_map/ppermute | solution.py:29
  41.3 66.4 %copy-start.19 = (f32[4,64,512]{2,1,0:T(8,128)}, f32[4,64,512]{2,1,0:T(8,128)S(1)}, u32[]{:S(2)}) copy-start(f32[4,64,512]{2,1,0:T(8,128)S(1)} %collective-permute-done.3.refs_4_) | copy-start | bytes 1572868
  41.3 22.0 %collective-permute-start.44 = (f32[4,64,512]{2,1,0:T(8,128)S(1)}, f32[4,64,512]{2,1,0:T(8,128)S(1)}, u32[]{:S(2)}, u32[]{:S(2)}) collective-permute-start(f32[4,64,512]{2,1,0:T(8,128)S(1)} %collective-permute-done.26.refs_2_), channel_id=1, source_target_pairs={{0,1},{1,0},{2,3},{3,2},{4,5},{5,4},{6,7},{7,6},{8,9},{9,8},{10,11... | collective-permute-start | bytes 1572872 | tf_op jit(solution)/shard_map/ppermute | solution.py:29
  41.3 66.5 %copy-start.21 = (f32[4,64,512]{2,1,0:T(8,128)}, f32[4,64,512]{2,1,0:T(8,128)S(1)}, u32[]{:S(2)}) copy-start(f32[4,64,512]{2,1,0:T(8,128)S(1)} %collective-permute-done.7.refs_8_) | copy-start | bytes 1572868
  41.3 23.9 %collective-permute-start.45 = (f32[4,64,512]{2,1,0:T(8,128)S(1)}, f32[4,64,512]{2,1,0:T(8,128)}, u32[]{:S(2)}, u32[]{:S(2)}) collective-permute-start(f32[4,64,512]{2,1,0:T(8,128)S(1)} %collective-permute-done.29.refs_4_), channel_id=1, source_target_pairs={{0,1},{1,0},{2,3},{3,2},{4,5},{5,4},{6,7},{7,6},{8,9},{9,8},{10,11... | collective-permute-start | bytes 1572872 | tf_op jit(solution)/shard_map/ppermute | solution.py:29
  41.8 24.5 %collective-permute-start.27 = (f32[4,64,512]{2,1,0:T(8,128)S(1)}, f32[4,64,512]{2,1,0:T(8,128)S(1)}, u32[]{:S(2)}, u32[]{:S(2)}) collective-permute-start(f32[4,64,512]{2,1,0:T(8,128)S(1)} %collective-permute-done.26.refs_2_), channel_id=1, source_target_pairs={{0,12},{1,13},{2,14},{3,15},{4,0},{5,1},{6,2},{7,3},{8,4},{9,5},{1... | collective-permute-start | bytes 1572872 | tf_op jit(solution)/shard_map/ppermute | solution.py:29
  42.7 134.5 %copy-start.1 = (f32[4,64,512]{2,1,0:T(8,128)}, f32[4,64,512]{2,1,0:T(8,128)S(1)}, u32[]{:S(2)}) copy-start(f32[4,64,512]{2,1,0:T(8,128)S(1)} %collective-permute-done.35.refs_8_) | copy-start | bytes 1572868
  42.7 25.1 %collective-permute-start.30 = (f32[4,64,512]{2,1,0:T(8,128)S(1)}, f32[4,64,512]{2,1,0:T(8,128)S(1)}, u32[]{:S(2)}, u32[]{:S(2)}) collective-permute-start(f32[4,64,512]{2,1,0:T(8,128)S(1)} %collective-permute-done.29.refs_4_), channel_id=1, source_target_pairs={{0,4},{1,5},{2,6},{3,7},{4,8},{5,9},{6,10},{7,11},{8,12},{9,13},{1... | collective-permute-start | bytes 1572872 | tf_op jit(solution)/shard_map/ppermute | solution.py:29
  54.4 80.0 %copy-start.25 = (f32[4,64,512]{2,1,0:T(8,128)}, f32[4,64,512]{2,1,0:T(8,128)S(1)}, u32[]{:S(2)}) copy-start(f32[4,64,512]{2,1,0:T(8,128)S(1)} %collective-permute-done.46.refs_6_) | copy-start | bytes 1572868
  54.4 13.4 %collective-permute-start.25 = (f32[4,64,512]{2,1,0:T(8,128)S(1)}, f32[4,64,512]{2,1,0:T(8,128)S(1)}, u32[]{:S(2)}, u32[]{:S(2)}) collective-permute-start(f32[4,64,512]{2,1,0:T(8,128)S(1)} %collective-permute-done.24.refs_0_), channel_id=1, source_target_pairs={{0,1},{1,0},{2,3},{3,2},{4,5},{5,4},{6,7},{7,6},{8,9},{9,8},{10,11... | collective-permute-start | bytes 1572872 | tf_op jit(solution)/shard_map/ppermute | solution.py:29
  63.3 12.8 %collective-permute-start.16 = (f32[4,64,512]{2,1,0:T(8,128)S(1)}, f32[4,64,512]{2,1,0:T(8,128)}, u32[]{:S(2)}, u32[]{:S(2)}) collective-permute-start(f32[4,64,512]{2,1,0:T(8,128)S(1)} %collective-permute-done.15), channel_id=1, source_target_pairs={{0,0},{1,4},{2,6},{3,2},{4,64},{5,68},{6,70},{7,66},{8,1},{9,5},{1... | collective-permute-start | bytes 1572872 | tf_op jit(solution)/shard_map/ppermute | solution.py:29
  65.2 15.1 %collective-permute-start.9 = (f32[4,64,512]{2,1,0:T(8,128)S(1)}, f32[4,64,512]{2,1,0:T(8,128)S(1)}, u32[]{:S(2)}, u32[]{:S(2)}) collective-permute-start(f32[4,64,512]{2,1,0:T(8,128)S(1)} %collective-permute-done.1.refs_2_), channel_id=1, source_target_pairs={{0,12},{1,13},{2,14},{3,15},{4,0},{5,1},{6,2},{7,3},{8,4},{9,5},{1... | collective-permute-start | bytes 1572872 | tf_op jit(solution)/shard_map/ppermute | solution.py:29
  66.3 121.5 %copy-start.2 = (f32[4,64,512]{2,1,0:T(8,128)}, f32[4,64,512]{2,1,0:T(8,128)S(1)}, u32[]{:S(2)}) copy-start(f32[4,64,512]{2,1,0:T(8,128)S(1)} %collective-permute-done.27.refs_2_) | copy-start | bytes 1572868
  66.3 21.1 %collective-permute-start.5 = (f32[4,64,512]{2,1,0:T(8,128)S(1)}, f32[4,64,512]{2,1,0:T(8,128)S(1)}, u32[]{:S(2)}, u32[]{:S(2)}) collective-permute-start(f32[4,64,512]{2,1,0:T(8,128)S(1)} %collective-permute-done.1.refs_2_), channel_id=1, source_target_pairs={{0,4},{1,5},{2,6},{3,7},{4,8},{5,9},{6,10},{7,11},{8,12},{9,13},{1... | collective-permute-start | bytes 1572872 | tf_op jit(solution)/shard_map/ppermute | solution.py:29
  67.8 120.0 %copy-start.3 = (f32[4,64,512]{2,1,0:T(8,128)}, f32[4,64,512]{2,1,0:T(8,128)S(1)}, u32[]{:S(2)}) copy-start(f32[4,64,512]{2,1,0:T(8,128)S(1)} %collective-permute-done.30.refs_4_) | copy-start | bytes 1572868
  67.8 30.4 %collective-permute-start.11 = (f32[4,64,512]{2,1,0:T(8,128)S(1)}, f32[4,64,512]{2,1,0:T(8,128)S(1)}, u32[]{:S(2)}, u32[]{:S(2)}) collective-permute-start(f32[4,64,512]{2,1,0:T(8,128)S(1)} %collective-permute-done.3.refs_4_), channel_id=1, source_target_pairs={{0,4},{1,5},{2,6},{3,7},{4,8},{5,9},{6,10},{7,11},{8,12},{9,13},{1... | collective-permute-start | bytes 1572872 | tf_op jit(solution)/shard_map/ppermute | solution.py:29
  67.8 120.0 %copy-start.4 = (f32[4,64,512]{2,1,0:T(8,128)}, f32[4,64,512]{2,1,0:T(8,128)S(1)}, u32[]{:S(2)}) copy-start(f32[4,64,512]{2,1,0:T(8,128)S(1)} %collective-permute-done.25.refs_1_) | copy-start | bytes 1572868
  67.8 38.4 %collective-permute-start.2 = (f32[4,64,512]{2,1,0:T(8,128)S(1)}, f32[4,64,512]{2,1,0:T(8,128)S(1)}, u32[]{:S(2)}, u32[]{:S(2)}) collective-permute-start(f32[4,64,512]{2,1,0:T(8,128)S(1)} %collective-permute-done.1.refs_2_), channel_id=1, source_target_pairs={{0,1},{1,0},{2,3},{3,2},{4,5},{5,4},{6,7},{7,6},{8,9},{9,8},{10,11... | collective-permute-start | bytes 1572872 | tf_op jit(solution)/shard_map/ppermute | solution.py:29
  76.1 30.2 %collective-permute-start.4 = (f32[4,64,512]{2,1,0:T(8,128)S(1)}, f32[4,64,512]{2,1,0:T(8,128)S(1)}, u32[]{:S(2)}, u32[]{:S(2)}) collective-permute-start(f32[4,64,512]{2,1,0:T(8,128)S(1)} %collective-permute-done.3.refs_4_), channel_id=1, source_target_pairs={{0,1},{1,0},{2,3},{3,2},{4,5},{5,4},{6,7},{7,6},{8,9},{9,8},{10,11... | collective-permute-start | bytes 1572872 | tf_op jit(solution)/shard_map/ppermute | solution.py:29
  80.3 27.3 %collective-permute-start.8 = (f32[4,64,512]{2,1,0:T(8,128)S(1)}, f32[4,64,512]{2,1,0:T(8,128)S(1)}, u32[]{:S(2)}, u32[]{:S(2)}) collective-permute-start(f32[4,64,512]{2,1,0:T(8,128)S(1)} %collective-permute-done.7.refs_8_), channel_id=1, source_target_pairs={{0,1},{1,0},{2,3},{3,2},{4,5},{5,4},{6,7},{7,6},{8,9},{9,8},{10,11... | collective-permute-start | bytes 1572872 | tf_op jit(solution)/shard_map/ppermute | solution.py:29
  87.3 20.4 %collective-permute-start.39 = (f32[4,64,512]{2,1,0:T(8,128)S(1)}, f32[4,64,512]{2,1,0:T(8,128)S(1)}, u32[]{:S(2)}, u32[]{:S(2)}) collective-permute-start(f32[4,64,512]{2,1,0:T(8,128)S(1)} %collective-permute-done.35.refs_8_), channel_id=1, source_target_pairs={{0,64},{1,65},{2,66},{3,67},{4,68},{5,69},{6,70},{7,71},{8,72},{9,... | collective-permute-start | bytes 1572872 | tf_op jit(solution)/shard_map/ppermute | solution.py:29
  98.2 18.3 %collective-permute-start.36 = (f32[4,64,512]{2,1,0:T(8,128)S(1)}, f32[4,64,512]{2,1,0:T(8,128)S(1)}, u32[]{:S(2)}, u32[]{:S(2)}) collective-permute-start(f32[4,64,512]{2,1,0:T(8,128)S(1)} %collective-permute-done.35.refs_8_), channel_id=1, source_target_pairs={{0,16},{1,17},{2,18},{3,19},{4,20},{5,21},{6,22},{7,23},{8,24},{9,... | collective-permute-start | bytes 1572872 | tf_op jit(solution)/shard_map/ppermute | solution.py:29
  106.2 12.7 %collective-permute-start.37 = (f32[4,64,512]{2,1,0:T(8,128)S(1)}, f32[4,64,512]{2,1,0:T(8,128)S(1)}, u32[]{:S(2)}, u32[]{:S(2)}) collective-permute-start(f32[4,64,512]{2,1,0:T(8,128)S(1)} %collective-permute-done.35.refs_8_), channel_id=1, source_target_pairs={{0,48},{1,49},{2,50},{3,51},{4,52},{5,53},{6,54},{7,55},{8,56},{9,... | collective-permute-start | bytes 1572872 | tf_op jit(solution)/shard_map/ppermute | solution.py:29
  106.3 66.4 %copy-start.31 = (f32[4,64,512]{2,1,0:T(8,128)}, f32[4,64,512]{2,1,0:T(8,128)S(1)}, u32[]{:S(2)}) copy-start(f32[4,64,512]{2,1,0:T(8,128)S(1)} %collective-permute-done.4.refs_5_) | copy-start | bytes 1572868
  106.3 12.6 %collective-permute-start.47 = (f32[4,64,512]{2,1,0:T(8,128)S(1)}, f32[4,64,512]{2,1,0:T(8,128)S(1)}, u32[]{:S(2)}, u32[]{:S(2)}) collective-permute-start(f32[4,64,512]{2,1,0:T(8,128)S(1)} %collective-permute-done.46.refs_6_), channel_id=1, source_target_pairs={{0,1},{1,0},{2,3},{3,2},{4,5},{5,4},{6,7},{7,6},{8,9},{9,8},{10,11... | collective-permute-start | bytes 1572872 | tf_op jit(solution)/shard_map/ppermute | solution.py:29
  107.7 14.2 %collective-permute-start.32 = (f32[4,64,512]{2,1,0:T(8,128)S(1)}, f32[4,64,512]{2,1,0:T(8,128)S(1)}, u32[]{:S(2)}, u32[]{:S(2)}) collective-permute-start(f32[4,64,512]{2,1,0:T(8,128)S(1)} %collective-permute-done.27.refs_2_), channel_id=1, source_target_pairs={{0,12},{1,13},{2,14},{3,15},{4,0},{5,1},{6,2},{7,3},{8,4},{9,5},{1... | collective-permute-start | bytes 1572872 | tf_op jit(solution)/shard_map/ppermute | solution.py:29
  107.8 69.4 %copy-start.5 = (f32[4,64,512]{2,1,0:T(8,128)}, f32[4,64,512]{2,1,0:T(8,128)S(1)}, u32[]{:S(2)}) copy-start(f32[4,64,512]{2,1,0:T(8,128)S(1)} %collective-permute-done.39.refs_12_) | copy-start | bytes 1572868
  107.8 14.1 %collective-permute-start.28 = (f32[4,64,512]{2,1,0:T(8,128)S(1)}, f32[4,64,512]{2,1,0:T(8,128)S(1)}, u32[]{:S(2)}, u32[]{:S(2)}) collective-permute-start(f32[4,64,512]{2,1,0:T(8,128)S(1)} %collective-permute-done.27.refs_2_), channel_id=1, source_target_pairs={{0,1},{1,0},{2,3},{3,2},{4,5},{5,4},{6,7},{7,6},{8,9},{9,8},{10,11... | collective-permute-start | bytes 1572872 | tf_op jit(solution)/shard_map/ppermute | solution.py:29
  116.5 6.7 %collective-permute-start.31 = (f32[4,64,512]{2,1,0:T(8,128)S(1)}, f32[4,64,512]{2,1,0:T(8,128)S(1)}, u32[]{:S(2)}, u32[]{:S(2)}) collective-permute-start(f32[4,64,512]{2,1,0:T(8,128)S(1)} %collective-permute-done.30.refs_4_), channel_id=1, source_target_pairs={{0,1},{1,0},{2,3},{3,2},{4,5},{5,4},{6,7},{7,6},{8,9},{9,8},{10,11... | collective-permute-start | bytes 1572872 | tf_op jit(solution)/shard_map/ppermute | solution.py:29
  118.8 15.5 %collective-permute-start.20 = (f32[4,64,512]{2,1,0:T(8,128)}, f32[4,64,512]{2,1,0:T(8,128)}, u32[]{:S(2)}, u32[]{:S(2)}) collective-permute-start(f32[4,64,512]{2,1,0:T(8,128)} %collective-permute-done.16.refs_16_), channel_id=1, source_target_pairs={{0,64},{1,65},{2,66},{3,67},{4,68},{5,69},{6,70},{7,71},{8,72},{9,... | collective-permute-start | bytes 1572872 | tf_op jit(solution)/shard_map/ppermute | solution.py:29
  118.9 15.5 %collective-permute-start.13 = (f32[4,64,512]{2,1,0:T(8,128)S(1)}, f32[4,64,512]{2,1,0:T(8,128)}, u32[]{:S(2)}, u32[]{:S(2)}) collective-permute-start(f32[4,64,512]{2,1,0:T(8,128)S(1)} %collective-permute-done.9.refs_10_), channel_id=1, source_target_pairs={{0,12},{1,13},{2,14},{3,15},{4,0},{5,1},{6,2},{7,3},{8,4},{9,5},{1... | collective-permute-start | bytes 1572872 | tf_op jit(solution)/shard_map/ppermute | solution.py:29
  121.8 16.0 %collective-permute-start.10 = (f32[4,64,512]{2,1,0:T(8,128)S(1)}, f32[4,64,512]{2,1,0:T(8,128)S(1)}, u32[]{:S(2)}, u32[]{:S(2)}) collective-permute-start(f32[4,64,512]{2,1,0:T(8,128)S(1)} %collective-permute-done.9.refs_10_), channel_id=1, source_target_pairs={{0,1},{1,0},{2,3},{3,2},{4,5},{5,4},{6,7},{7,6},{8,9},{9,8},{10,11... | collective-permute-start | bytes 1572872 | tf_op jit(solution)/shard_map/ppermute | solution.py:29
  121.8 16.2 %collective-permute-start.17 = (f32[4,64,512]{2,1,0:T(8,128)}, f32[4,64,512]{2,1,0:T(8,128)}, u32[]{:S(2)}, u32[]{:S(2)}) collective-permute-start(f32[4,64,512]{2,1,0:T(8,128)} %collective-permute-done.16.refs_16_), channel_id=1, source_target_pairs={{0,16},{1,17},{2,18},{3,19},{4,20},{5,21},{6,22},{7,23},{8,24},{9,... | collective-permute-start | bytes 1572872 | tf_op jit(solution)/shard_map/ppermute | solution.py:29
  123.2 15.0 %collective-permute-start.6 = (f32[4,64,512]{2,1,0:T(8,128)S(1)}, f32[4,64,512]{2,1,0:T(8,128)S(1)}, u32[]{:S(2)}, u32[]{:S(2)}) collective-permute-start(f32[4,64,512]{2,1,0:T(8,128)S(1)} %collective-permute-done.5.refs_6_), channel_id=1, source_target_pairs={{0,1},{1,0},{2,3},{3,2},{4,5},{5,4},{6,7},{7,6},{8,9},{9,8},{10,11... | collective-permute-start | bytes 1572872 | tf_op jit(solution)/shard_map/ppermute | solution.py:29
  134.3 4.1 %collective-permute-start.12 = (f32[4,64,512]{2,1,0:T(8,128)S(1)}, f32[4,64,512]{2,1,0:T(8,128)S(1)}, u32[]{:S(2)}, u32[]{:S(2)}) collective-permute-start(f32[4,64,512]{2,1,0:T(8,128)S(1)} %collective-permute-done.11.refs_12_), channel_id=1, source_target_pairs={{0,1},{1,0},{2,3},{3,2},{4,5},{5,4},{6,7},{7,6},{8,9},{9,8},{10,11... | collective-permute-start | bytes 1572872 | tf_op jit(solution)/shard_map/ppermute | solution.py:29
  134.3 15.8 %collective-permute-start.41 = (f32[4,64,512]{2,1,0:T(8,128)S(1)}, f32[4,64,512]{2,1,0:T(8,128)S(1)}, u32[]{:S(2)}, u32[]{:S(2)}) collective-permute-start(f32[4,64,512]{2,1,0:T(8,128)S(1)} %collective-permute-done.39.refs_12_), channel_id=1, source_target_pairs={{0,48},{1,49},{2,50},{3,51},{4,52},{5,53},{6,54},{7,55},{8,56},{9,... | collective-permute-start | bytes 1572872 | tf_op jit(solution)/shard_map/ppermute | solution.py:29
  137.8 16.3 %collective-permute-start.40 = (f32[4,64,512]{2,1,0:T(8,128)S(1)}, f32[4,64,512]{2,1,0:T(8,128)S(1)}, u32[]{:S(2)}, u32[]{:S(2)}) collective-permute-start(f32[4,64,512]{2,1,0:T(8,128)S(1)} %collective-permute-done.39.refs_12_), channel_id=1, source_target_pairs={{0,16},{1,17},{2,18},{3,19},{4,20},{5,21},{6,22},{7,23},{8,24},{9,... | collective-permute-start | bytes 1572872 | tf_op jit(solution)/shard_map/ppermute | solution.py:29
  138.1 26.4 %collective-permute-start.38 = (f32[4,64,512]{2,1,0:T(8,128)S(1)}, f32[4,64,512]{2,1,0:T(8,128)S(1)}, u32[]{:S(2)}, u32[]{:S(2)}) collective-permute-start(f32[4,64,512]{2,1,0:T(8,128)S(1)} %collective-permute-done.36.refs_9_), channel_id=1, source_target_pairs={{0,16},{1,17},{2,18},{3,19},{4,20},{5,21},{6,22},{7,23},{8,24},{9,... | collective-permute-start | bytes 1572872 | tf_op jit(solution)/shard_map/ppermute | solution.py:29
  138.2 26.3 %collective-permute-start.33 = (f32[4,64,512]{2,1,0:T(8,128)S(1)}, f32[4,64,512]{2,1,0:T(8,128)S(1)}, u32[]{:S(2)}, u32[]{:S(2)}) collective-permute-start(f32[4,64,512]{2,1,0:T(8,128)S(1)} %collective-permute-done.32.refs_6_), channel_id=1, source_target_pairs={{0,1},{1,0},{2,3},{3,2},{4,5},{5,4},{6,7},{7,6},{8,9},{9,8},{10,11... | collective-permute-start | bytes 1572872 | tf_op jit(solution)/shard_map/ppermute | solution.py:29
  138.5 26.2 %collective-permute-start.22 = (f32[4,64,512]{2,1,0:T(8,128)}, f32[4,64,512]{2,1,0:T(8,128)}, u32[]{:S(2)}, u32[]{:S(2)}) collective-permute-start(f32[4,64,512]{2,1,0:T(8,128)} %collective-permute-done.20.refs_20_), channel_id=1, source_target_pairs={{0,48},{1,49},{2,50},{3,51},{4,52},{5,53},{6,54},{7,55},{8,56},{9,... | collective-permute-start | bytes 1572872 | tf_op jit(solution)/shard_map/ppermute | solution.py:29
  150.1 22.5 %collective-permute-start.42 = (f32[4,64,512]{2,1,0:T(8,128)S(1)}, f32[4,64,512]{2,1,0:T(8,128)S(1)}, u32[]{:S(2)}, u32[]{:S(2)}) collective-permute-start(f32[4,64,512]{2,1,0:T(8,128)S(1)} %collective-permute-done.41.refs_14_), channel_id=1, source_target_pairs={{0,48},{1,49},{2,50},{3,51},{4,52},{5,53},{6,54},{7,55},{8,56},{9,... | collective-permute-start | bytes 1572872 | tf_op jit(solution)/shard_map/ppermute | solution.py:29
  154.1 44.3 %collective-permute-start.18 = (f32[4,64,512]{2,1,0:T(8,128)}, f32[4,64,512]{2,1,0:T(8,128)}, u32[]{:S(2)}, u32[]{:S(2)}) collective-permute-start(f32[4,64,512]{2,1,0:T(8,128)} %collective-permute-done.16.refs_16_), channel_id=1, source_target_pairs={{0,48},{1,49},{2,50},{3,51},{4,52},{5,53},{6,54},{7,55},{8,56},{9,... | collective-permute-start | bytes 1572872 | tf_op jit(solution)/shard_map/ppermute | solution.py:29
  164.5 33.9 %collective-permute-start.21 = (f32[4,64,512]{2,1,0:T(8,128)}, f32[4,64,512]{2,1,0:T(8,128)}, u32[]{:S(2)}, u32[]{:S(2)}) collective-permute-start(f32[4,64,512]{2,1,0:T(8,128)} %collective-permute-done.20.refs_20_), channel_id=1, source_target_pairs={{0,16},{1,17},{2,18},{3,19},{4,20},{5,21},{6,22},{7,23},{8,24},{9,... | collective-permute-start | bytes 1572872 | tf_op jit(solution)/shard_map/ppermute | solution.py:29
  164.6 33.9 %collective-permute-start.14 = (f32[4,64,512]{2,1,0:T(8,128)}, f32[4,64,512]{2,1,0:T(8,128)}, u32[]{:S(2)}, u32[]{:S(2)}) collective-permute-start(f32[4,64,512]{2,1,0:T(8,128)} %collective-permute-done.13.refs_14_), channel_id=1, source_target_pairs={{0,1},{1,0},{2,3},{3,2},{4,5},{5,4},{6,7},{7,6},{8,9},{9,8},{10,11... | collective-permute-start | bytes 1572872 | tf_op jit(solution)/shard_map/ppermute | solution.py:29
  164.7 33.8 %collective-permute-start.19 = (f32[4,64,512]{2,1,0:T(8,128)}, f32[4,64,512]{2,1,0:T(8,128)}, u32[]{:S(2)}, u32[]{:S(2)}) collective-permute-start(f32[4,64,512]{2,1,0:T(8,128)} %collective-permute-done.17.refs_17_), channel_id=1, source_target_pairs={{0,16},{1,17},{2,18},{3,19},{4,20},{5,21},{6,22},{7,23},{8,24},{9,... | collective-permute-start | bytes 1572872 | tf_op jit(solution)/shard_map/ppermute | solution.py:29
  173.5 24.9 %collective-permute-start.23 = (f32[4,64,512]{2,1,0:T(8,128)}, f32[4,64,512]{2,1,0:T(8,128)}, u32[]{:S(2)}, u32[]{:S(2)}) collective-permute-start(f32[4,64,512]{2,1,0:T(8,128)} %collective-permute-done.22.refs_22_), channel_id=1, source_target_pairs={{0,48},{1,49},{2,50},{3,51},{4,52},{5,53},{6,54},{7,55},{8,56},{9,... | collective-permute-start | bytes 1572872 | tf_op jit(solution)/shard_map/ppermute | solution.py:29
  (21 other events, 708.9 us)

commit v3 on v2

--- a/solution.py
+++ b/solution.py
@@ -43,7 +43,7 @@
     return [(chunk, move(chunk, swap)) for chunk in chunks]
 
 
-def gather_columns(own):
+def gather_columns(tag, own):
     step_z = lambda d: lambda x, h, l, z, k: (x, h, l, z + d, k)
     shifted = move(own, lambda x, h, l, z, k: (x, h, l, z + 2 * k + l, k))
 
@@ -58,7 +58,11 @@
     other_minus = move(other, step_z(1))
     other_plus = move(other, step_z(-1))
     entry_far = move(entry_minus, step_z(1))
-    other_far = move(other_plus, step_z(-1))
+    if tag == "0":
+        other_far = move(other_plus, step_z(-1))
+    else:
+        partner = lambda x, h, l, z, k: (x, h + 1, l, z, k)
+        other_far = move(entry_far, partner)
     return (
         (entry, entry_minus, entry_plus, entry_far),
         (other, other_minus, other_plus, other_far),
@@ -214,7 +218,7 @@
         )
         for s, d in PIECES
     ]
-    columns = [gather_columns(part) for part in parts]
+    columns = [gather_columns(str(n), part) for n, part in enumerate(parts)]
     tiles = [gather_rows(part) for part in parts]
     density = None
     for n, (entry, other) in enumerate(columns):

time: 218 us -> 221 us (1.014)
  the two profiles are of different devices: /device:TPU:8 before, /device:TPU:1 now
where the time goes in v3:
time: 221 us
  waiting for transfers between devices  99.1 us (45%)
  starting transfers between devices  77.8 us (35%)
  Pallas kernels  40.3 us (18%)
  local copies, waits for them, and re-layouts  3.09 us (1%)
    ppermute x48, waiting for transfers between devices, move(): return lax.ppermute(value, AXES, pairs)  99.1 us
    ppermute x48, starting transfers between devices, move(): return lax.ppermute(value, AXES, pairs)  77.8 us
    pallas_call x3, Pallas kernels, add_tiles(): pl.pallas_call(functools.partial(density_kernel, add, first, tiles), out_...  40.3 us
  transfers between devices with their start and end apart: 48, of which 17 were waited for; matrix products, arithmetic and copies ran while one was open for 0% of the time, Pallas kernels for 10%

profile of v3, /device:TPU:1, one launch (start us, length us, event | category | flops | bytes accessed | tf_op | source)
XLA Modules:
  0.0 221.1 jit_solution(6406388478855282707)
XLA Ops:
  0.0 1.2 fusion
  1.2 1.0 slice_bitcast_fusion
  2.2 6.3 %collective-permute-start.34 = (f32[4,64,512]{2,1,0:T(8,128)S(1)}, f32[4,64,512]{2,1,0:T(8,128)S(1)}, u32[]{:S(2)}, u32[]{:S(2)}) collective-permute-start(f32[4,64,512]{2,1,0:T(8,128)S(1)} %pad_maximum_fusion.1.refs_0_), channel_id=1, source_target_pairs={{0,0},{1,33},{2,18},{3,51},{4,4},{5,37},{6,22},{7,55},{8,8},{9,41}... | collective-permute-start | bytes 1572872 | tf_op jit(solution)/shard_map/ppermute | solution.py:29
  8.5 1.5 collective-permute-start.26
  10.1 1.2 collective-permute-start.29
  11.3 1.5 collective-permute-start.24
  12.8 2.3 %collective-permute-done.34 = f32[4,64,512]{2,1,0:T(8,128)S(1)} collective-permute-done((f32[4,64,512]{2,1,0:T(8,128)S(1)}, f32[4,64,512]{2,1,0:T(8,128)S(1)}, u32[]{:S(2)}, u32[]{:S(2)}) %collective-permute-start.34) | collective-permute-done | bytes 524320 | tf_op jit(solution)/shard_map/ppermute | solution.py:29
  15.1 1.0 collective-permute-start.1
  16.1 6.5 %collective-permute-done.26.refs_2_ = f32[4,64,512]{2,1,0:T(8,128)S(1)} collective-permute-done((f32[4,64,512]{2,1,0:T(8,128)S(1)}, f32[4,64,512]{2,1,0:T(8,128)S(1)}, u32[]{:S(2)}, u32[]{:S(2)}) %collective-permute-start.26) | collective-permute-done | bytes 524320 | tf_op jit(solution)/shard_map/ppermute | solution.py:29
  22.6 1.9 collective-permute-start.15
  24.5 0.0 collective-permute-done.29.refs_4_
  24.5 1.3 collective-permute-start.3
  25.8 1.5 collective-permute-start.7
  27.3 0.8 collective-permute-start
  28.0 4.8 %collective-permute-done.1.refs_2_ = f32[4,64,512]{2,1,0:T(8,128)S(1)} collective-permute-done((f32[4,64,512]{2,1,0:T(8,128)S(1)}, f32[4,64,512]{2,1,0:T(8,128)S(1)}, u32[]{:S(2)}, u32[]{:S(2)}) %collective-permute-start.1) | collective-permute-done | bytes 524320 | tf_op jit(solution)/shard_map/ppermute | solution.py:29
  32.8 2.4 %collective-permute-start.35 = (f32[4,64,512]{2,1,0:T(8,128)S(1)}, f32[4,64,512]{2,1,0:T(8,128)S(1)}, u32[]{:S(2)}, u32[]{:S(2)}) collective-permute-start(f32[4,64,512]{2,1,0:T(8,128)S(1)} %collective-permute-done.34), channel_id=1, source_target_pairs={{0,0},{1,4},{2,6},{3,2},{4,64},{5,68},{6,70},{7,66},{8,1},{9,5},{1... | collective-permute-start | bytes 1572872 | tf_op jit(solution)/shard_map/ppermute | solution.py:29
  35.2 2.5 %collective-permute-start.46 = (f32[4,64,512]{2,1,0:T(8,128)S(1)}, f32[4,64,512]{2,1,0:T(8,128)S(1)}, u32[]{:S(2)}, u32[]{:S(2)}) collective-permute-start(f32[4,64,512]{2,1,0:T(8,128)S(1)} %collective-permute-done.26.refs_2_), channel_id=1, source_target_pairs={{0,4},{1,5},{2,6},{3,7},{4,8},{5,9},{6,10},{7,11},{8,12},{9,13},{1... | collective-permute-start | bytes 1572872 | tf_op jit(solution)/shard_map/ppermute | solution.py:29
  37.7 1.3 collective-permute-done.3.refs_4_
  39.1 1.2 collective-permute-start.44
  40.2 0.1 collective-permute-start.45
  40.3 2.5 %collective-permute-start.27 = (f32[4,64,512]{2,1,0:T(8,128)S(1)}, f32[4,64,512]{2,1,0:T(8,128)S(1)}, u32[]{:S(2)}, u32[]{:S(2)}) collective-permute-start(f32[4,64,512]{2,1,0:T(8,128)S(1)} %collective-permute-done.26.refs_2_), channel_id=1, source_target_pairs={{0,12},{1,13},{2,14},{3,15},{4,0},{5,1},{6,2},{7,3},{8,4},{9,5},{1... | collective-permute-start | bytes 1572872 | tf_op jit(solution)/shard_map/ppermute | solution.py:29
  42.8 5.3 %collective-permute-done.35.refs_8_ = f32[4,64,512]{2,1,0:T(8,128)S(1)} collective-permute-done((f32[4,64,512]{2,1,0:T(8,128)S(1)}, f32[4,64,512]{2,1,0:T(8,128)S(1)}, u32[]{:S(2)}, u32[]{:S(2)}) %collective-permute-start.35) | collective-permute-done | bytes 524320 | tf_op jit(solution)/shard_map/ppermute | solution.py:29
  48.1 7.5 %collective-permute-start.30 = (f32[4,64,512]{2,1,0:T(8,128)S(1)}, f32[4,64,512]{2,1,0:T(8,128)S(1)}, u32[]{:S(2)}, u32[]{:S(2)}) collective-permute-start(f32[4,64,512]{2,1,0:T(8,128)S(1)} %collective-permute-done.29.refs_4_), channel_id=1, source_target_pairs={{0,4},{1,5},{2,6},{3,7},{4,8},{5,9},{6,10},{7,11},{8,12},{9,13},{1... | collective-permute-start | bytes 1572872 | tf_op jit(solution)/shard_map/ppermute | solution.py:29
  55.7 1.7 collective-permute-done.46.refs_6_
  57.4 11.2 %collective-permute-start.25 = (f32[4,64,512]{2,1,0:T(8,128)S(1)}, f32[4,64,512]{2,1,0:T(8,128)S(1)}, u32[]{:S(2)}, u32[]{:S(2)}) collective-permute-start(f32[4,64,512]{2,1,0:T(8,128)S(1)} %collective-permute-done.24.refs_0_), channel_id=1, source_target_pairs={{0,1},{1,0},{2,3},{3,2},{4,5},{5,4},{6,7},{7,6},{8,9},{9,8},{10,11... | collective-permute-start | bytes 1572872 | tf_op jit(solution)/shard_map/ppermute | solution.py:29
  68.6 3.6 %collective-permute-start.16 = (f32[4,64,512]{2,1,0:T(8,128)S(1)}, f32[4,64,512]{2,1,0:T(8,128)}, u32[]{:S(2)}, u32[]{:S(2)}) collective-permute-start(f32[4,64,512]{2,1,0:T(8,128)S(1)} %collective-permute-done.15), channel_id=1, source_target_pairs={{0,0},{1,4},{2,6},{3,2},{4,64},{5,68},{6,70},{7,66},{8,1},{9,5},{1... | collective-permute-start | bytes 1572872 | tf_op jit(solution)/shard_map/ppermute | solution.py:29
  72.3 0.1 collective-permute-start.5
  72.4 1.2 collective-permute-start.11
  73.6 0.8 collective-permute-start.2
  74.4 7.6 %collective-permute-done.9.refs_10_ = f32[4,64,512]{2,1,0:T(8,128)S(1)} collective-permute-done((f32[4,64,512]{2,1,0:T(8,128)S(1)}, f32[4,64,512]{2,1,0:T(8,128)S(1)}, u32[]{:S(2)}, u32[]{:S(2)}) %collective-permute-start.9) | collective-permute-done | bytes 524320 | tf_op jit(solution)/shard_map/ppermute | solution.py:29
  82.0 0.9 collective-permute-start.4
  83.0 3.4 %collective-permute-done.16.refs_16_ = f32[4,64,512]{2,1,0:T(8,128)} collective-permute-done((f32[4,64,512]{2,1,0:T(8,128)S(1)}, f32[4,64,512]{2,1,0:T(8,128)}, u32[]{:S(2)}, u32[]{:S(2)}) %collective-permute-start.16) | collective-permute-done | bytes 524320 | tf_op jit(solution)/shard_map/ppermute | solution.py:29
  86.4 8.1 %collective-permute-done.5.refs_6_ = f32[4,64,512]{2,1,0:T(8,128)S(1)} collective-permute-done((f32[4,64,512]{2,1,0:T(8,128)S(1)}, f32[4,64,512]{2,1,0:T(8,128)S(1)}, u32[]{:S(2)}, u32[]{:S(2)}) %collective-permute-start.5) | collective-permute-done | bytes 524320 | tf_op jit(solution)/shard_map/ppermute | solution.py:29
  94.5 9.4 %collective-permute-done.11.refs_12_ = f32[4,64,512]{2,1,0:T(8,128)S(1)} collective-permute-done((f32[4,64,512]{2,1,0:T(8,128)S(1)}, f32[4,64,512]{2,1,0:T(8,128)S(1)}, u32[]{:S(2)}, u32[]{:S(2)}) %collective-permute-start.11) | collective-permute-done | bytes 524320 | tf_op jit(solution)/shard_map/ppermute | solution.py:29
  103.9 1.6 collective-permute-start.36
  105.5 3.1 %collective-permute-start.37 = (f32[4,64,512]{2,1,0:T(8,128)S(1)}, f32[4,64,512]{2,1,0:T(8,128)S(1)}, u32[]{:S(2)}, u32[]{:S(2)}) collective-permute-start(f32[4,64,512]{2,1,0:T(8,128)S(1)} %collective-permute-done.35.refs_8_), channel_id=1, source_target_pairs={{0,48},{1,49},{2,50},{3,51},{4,52},{5,53},{6,54},{7,55},{8,56},{9,... | collective-permute-start | bytes 1572872 | tf_op jit(solution)/shard_map/ppermute | solution.py:29
  108.6 2.7 %collective-permute-start.47 = (f32[4,64,512]{2,1,0:T(8,128)S(1)}, f32[4,64,512]{2,1,0:T(8,128)}, u32[]{:S(2)}, u32[]{:S(2)}) collective-permute-start(f32[4,64,512]{2,1,0:T(8,128)S(1)} %collective-permute-done.46.refs_6_), channel_id=1, source_target_pairs={{0,1},{1,0},{2,3},{3,2},{4,5},{5,4},{6,7},{7,6},{8,9},{9,8},{10,11... | collective-permute-start | bytes 1572872 | tf_op jit(solution)/shard_map/ppermute | solution.py:29
  111.3 0.1 collective-permute-start.32
  111.4 0.1 collective-permute-start.28
  111.5 6.8 %collective-permute-done.36.refs_9_ = f32[4,64,512]{2,1,0:T(8,128)S(1)} collective-permute-done((f32[4,64,512]{2,1,0:T(8,128)S(1)}, f32[4,64,512]{2,1,0:T(8,128)S(1)}, u32[]{:S(2)}, u32[]{:S(2)}) %collective-permute-start.36) | collective-permute-done | bytes 524320 | tf_op jit(solution)/shard_map/ppermute | solution.py:29
  118.4 3.0 %collective-permute-start.31 = (f32[4,64,512]{2,1,0:T(8,128)S(1)}, f32[4,64,512]{2,1,0:T(8,128)S(1)}, u32[]{:S(2)}, u32[]{:S(2)}) collective-permute-start(f32[4,64,512]{2,1,0:T(8,128)S(1)} %collective-permute-done.30.refs_4_), channel_id=1, source_target_pairs={{0,1},{1,0},{2,3},{3,2},{4,5},{5,4},{6,7},{7,6},{8,9},{9,8},{10,11... | collective-permute-start | bytes 1572872 | tf_op jit(solution)/shard_map/ppermute | solution.py:29
  121.4 0.1 collective-permute-start.17
  121.5 3.3 %collective-permute-done.32.refs_6_ = f32[4,64,512]{2,1,0:T(8,128)S(1)} collective-permute-done((f32[4,64,512]{2,1,0:T(8,128)S(1)}, f32[4,64,512]{2,1,0:T(8,128)S(1)}, u32[]{:S(2)}, u32[]{:S(2)}) %collective-permute-start.32) | collective-permute-done | bytes 524320 | tf_op jit(solution)/shard_map/ppermute | solution.py:29
  124.8 1.5 collective-permute-start.10
  126.3 0.1 collective-permute-start.6
  126.4 9.7 %collective-permute-done.13.refs_14_ = f32[4,64,512]{2,1,0:T(8,128)} collective-permute-done((f32[4,64,512]{2,1,0:T(8,128)S(1)}, f32[4,64,512]{2,1,0:T(8,128)}, u32[]{:S(2)}, u32[]{:S(2)}) %collective-permute-start.13) | collective-permute-done | bytes 524320 | tf_op jit(solution)/shard_map/ppermute | solution.py:29
  136.2 0.9 collective-permute-start.12
  137.1 0.1 collective-permute-start.41
  137.1 1.6 collective-permute-done.20.refs_20_
  138.7 0.0 collective-permute-start.40
  138.8 0.1 collective-permute-start.38
  138.9 2.3 %collective-permute-start.33 = (f32[4,64,512]{2,1,0:T(8,128)S(1)}, f32[4,64,512]{2,1,0:T(8,128)S(1)}, u32[]{:S(2)}, u32[]{:S(2)}) collective-permute-start(f32[4,64,512]{2,1,0:T(8,128)S(1)} %collective-permute-done.32.refs_6_), channel_id=1, source_target_pairs={{0,1},{1,0},{2,3},{3,2},{4,5},{5,4},{6,7},{7,6},{8,9},{9,8},{10,11... | collective-permute-start | bytes 1572872 | tf_op jit(solution)/shard_map/ppermute | solution.py:29
  141.2 1.2 collective-permute-start.19
  142.4 8.1 %collective-permute-done.41.refs_14_ = f32[4,64,512]{2,1,0:T(8,128)S(1)} collective-permute-done((f32[4,64,512]{2,1,0:T(8,128)S(1)}, f32[4,64,512]{2,1,0:T(8,128)S(1)}, u32[]{:S(2)}, u32[]{:S(2)}) %collective-permute-start.41) | collective-permute-done | bytes 524320 | tf_op jit(solution)/shard_map/ppermute | solution.py:29
  150.5 1.5 collective-permute-start.42
  152.0 0.1 collective-permute-start.18
  152.1 10.4 %collective-permute-done.38.refs_11_ = f32[4,64,512]{2,1,0:T(8,128)S(1)} collective-permute-done((f32[4,64,512]{2,1,0:T(8,128)S(1)}, f32[4,64,512]{2,1,0:T(8,128)S(1)}, u32[]{:S(2)}, u32[]{:S(2)}) %collective-permute-start.38) | collective-permute-done | bytes 524320 | tf_op jit(solution)/shard_map/ppermute | solution.py:29
  162.5 2.7 %collective-permute-start.22 = (f32[4,64,512]{2,1,0:T(8,128)}, f32[4,64,512]{2,1,0:T(8,128)}, u32[]{:S(2)}, u32[]{:S(2)}) collective-permute-start(f32[4,64,512]{2,1,0:T(8,128)} %collective-permute-done.20.refs_20_), channel_id=1, source_target_pairs={{0,48},{1,49},{2,50},{3,51},{4,52},{5,53},{6,54},{7,55},{8,56},{9,... | collective-permute-start | bytes 1572872 | tf_op jit(solution)/shard_map/ppermute | solution.py:29
  165.2 8.6 %collective-permute-done.19.refs_19_ = f32[4,64,512]{2,1,0:T(8,128)} collective-permute-done((f32[4,64,512]{2,1,0:T(8,128)S(1)}, f32[4,64,512]{2,1,0:T(8,128)}, u32[]{:S(2)}, u32[]{:S(2)}) %collective-permute-start.19) | collective-permute-done | bytes 524320 | tf_op jit(solution)/shard_map/ppermute | solution.py:29
  173.8 5.8 %collective-permute-start.14 = (f32[4,64,512]{2,1,0:T(8,128)}, f32[4,64,512]{2,1,0:T(8,128)}, u32[]{:S(2)}, u32[]{:S(2)}) collective-permute-start(f32[4,64,512]{2,1,0:T(8,128)} %collective-permute-done.13.refs_14_), channel_id=1, source_target_pairs={{0,1},{1,0},{2,3},{3,2},{4,5},{5,4},{6,7},{7,6},{8,9},{9,8},{10,11... | collective-permute-start | bytes 1572872 | tf_op jit(solution)/shard_map/ppermute | solution.py:29
  179.7 0.8 copy-done.15
  180.5 10.6 %shard_map.28.refs_16_ = f32[3,1024,512]{2,1,0:T(8,128)} custom-call(f32[4,64,512]{2,1,0:T(8,128)} %copy-done.17, f32[4,64,512]{2,1,0:T(8,128)} %copy-done.23, f32[4,64,512]{2,1,0:T(8,128)} %copy-done.20, f32[4,64,512]{2,1,0:T(8,128)} %copy-done.27, f32[4,64,512]{2,1,0:T(8,128)} %copy-done.22, f32[4,64,512]{2,1,0:T(8,128)} %copy-done.28, ...), custom_call_target="tpu_custom_call" | custom-call | flops 4831838208 | bytes 8388608 | tf_op jit(solution)/shard_map/pallas_call | solution.py:182
  191.1 10.6 %shard_map.29.refs_24_ = f32[3,1024,512]{2,1,0:T(8,128)} custom-call(f32[4,64,512]{2,1,0:T(8,128)} %copy-done, f32[4,64,512]{2,1,0:T(8,128)} %copy-done.4, f32[4,64,512]{2,1,0:T(8,128)} %copy-done.2, f32[4,64,512]{2,1,0:T(8,128)} %copy-done.9, f32[4,64,512]{2,1,0:T(8,128)} %copy-done.3, f32[4,64,512]{2,1,0:T(8,128)} %copy-done.10, ...), custom_call_target="tpu_custom_call", output_to_operand_aliasing={{}: (16, {})} | custom-call | flops 4831838208 | bytes 8388608 | tf_op jit(solution)/shard_map/pallas_call | solution.py:182
  201.8 19.1 %shard_map.30 = f32[3,1024,512]{2,1,0:T(8,128)} custom-call(f32[4,64,512]{2,1,0:T(8,128)} %copy-done.16, f32[4,64,512]{2,1,0:T(8,128)} %copy-done.24, f32[4,64,512]{2,1,0:T(8,128)} %copy-done.18, f32[4,64,512]{2,1,0:T(8,128)} %copy-done.31, f32[4,64,512]{2,1,0:T(8,128)} %copy-done.19, f32[4,64,512]{2,1,0:T(8,128)} %copy-done.32, ...), custom_call_target="tpu_custom_call", output_to_operand_aliasing={{}: (24, {})} | custom-call | flops 9663676416 | bytes 12582912 | tf_op jit(solution)/shard_map/pallas_call | solution.py:182
  (115 shorter events, 0.3 us)
Async XLA Ops:
  2.2 177.4 %copy-start.17 = (f32[4,64,512]{2,1,0:T(8,128)}, f32[4,64,512]{2,1,0:T(8,128)S(1)}, u32[]{:S(2)}) copy-start(f32[4,64,512]{2,1,0:T(8,128)S(1)} %pad_maximum_fusion.1.refs_0_) | copy-start | bytes 1572868
  2.2 12.9 %collective-permute-start.34 = (f32[4,64,512]{2,1,0:T(8,128)S(1)}, f32[4,64,512]{2,1,0:T(8,128)S(1)}, u32[]{:S(2)}, u32[]{:S(2)}) collective-permute-start(f32[4,64,512]{2,1,0:T(8,128)S(1)} %pad_maximum_fusion.1.refs_0_), channel_id=1, source_target_pairs={{0,0},{1,33},{2,18},{3,51},{4,4},{5,37},{6,22},{7,55},{8,8},{9,41}... | collective-permute-start | bytes 1572872 | tf_op jit(solution)/shard_map/ppermute | solution.py:29
  8.5 14.0 %collective-permute-start.26 = (f32[4,64,512]{2,1,0:T(8,128)S(1)}, f32[4,64,512]{2,1,0:T(8,128)S(1)}, u32[]{:S(2)}, u32[]{:S(2)}) collective-permute-start(f32[4,64,512]{2,1,0:T(8,128)S(1)} %pad_maximum_fusion.1.refs_0_), channel_id=1, source_target_pairs={{0,2},{1,3},{2,0},{3,1},{4,6},{5,7},{6,4},{7,5},{8,10},{9,11},{10,... | collective-permute-start | bytes 1572872 | tf_op jit(solution)/shard_map/ppermute | solution.py:29
  10.1 14.4 %collective-permute-start.29 = (f32[4,64,512]{2,1,0:T(8,128)S(1)}, f32[4,64,512]{2,1,0:T(8,128)S(1)}, u32[]{:S(2)}, u32[]{:S(2)}) collective-permute-start(f32[4,64,512]{2,1,0:T(8,128)S(1)} %pad_maximum_fusion.1.refs_0_), channel_id=1, source_target_pairs={{0,4},{1,5},{2,6},{3,7},{4,8},{5,9},{6,10},{7,11},{8,12},{9,13},{1... | collective-permute-start | bytes 1572872 | tf_op jit(solution)/shard_map/ppermute | solution.py:29
  11.3 14.5 %collective-permute-start.43 = (f32[4,64,512]{2,1,0:T(8,128)S(1)}, f32[4,64,512]{2,1,0:T(8,128)S(1)}, u32[]{:S(2)}, u32[]{:S(2)}) collective-permute-start(f32[4,64,512]{2,1,0:T(8,128)S(1)} %pad_maximum_fusion.1.refs_0_), channel_id=1, source_target_pairs={{0,1},{1,0},{2,3},{3,2},{4,5},{5,4},{6,7},{7,6},{8,9},{9,8},{10,11... | collective-permute-start | bytes 1572872 | tf_op jit(solution)/shard_map/ppermute | solution.py:29
  11.3 16.0 %collective-permute-start.24 = (f32[4,64,512]{2,1,0:T(8,128)S(1)}, f32[4,64,512]{2,1,0:T(8,128)S(1)}, u32[]{:S(2)}, u32[]{:S(2)}) collective-permute-start(f32[4,64,512]{2,1,0:T(8,128)S(1)} %pad_maximum_fusion.1.refs_0_), channel_id=1, source_target_pairs={{0,12},{1,13},{2,14},{3,15},{4,0},{5,1},{6,2},{7,3},{8,4},{9,5},{1... | collective-permute-start | bytes 1572872 | tf_op jit(solution)/shard_map/ppermute | solution.py:29
  12.8 166.8 %copy-start.16 = (f32[4,64,512]{2,1,0:T(8,128)}, f32[4,64,512]{2,1,0:T(8,128)S(1)}, u32[]{:S(2)}) copy-start(f32[4,64,512]{2,1,0:T(8,128)S(1)} %pad_maximum_fusion.refs_0_) | copy-start | bytes 1572868
  15.1 17.7 %collective-permute-start.1 = (f32[4,64,512]{2,1,0:T(8,128)S(1)}, f32[4,64,512]{2,1,0:T(8,128)S(1)}, u32[]{:S(2)}, u32[]{:S(2)}) collective-permute-start(f32[4,64,512]{2,1,0:T(8,128)S(1)} %pad_maximum_fusion.refs_0_), channel_id=1, source_target_pairs={{0,2},{1,3},{2,0},{3,1},{4,6},{5,7},{6,4},{7,5},{8,10},{9,11},{10,... | collective-permute-start | bytes 1572872 | tf_op jit(solution)/shard_map/ppermute | solution.py:29
  22.6 157.0 %copy-start.20 = (f32[4,64,512]{2,1,0:T(8,128)}, f32[4,64,512]{2,1,0:T(8,128)S(1)}, u32[]{:S(2)}) copy-start(f32[4,64,512]{2,1,0:T(8,128)S(1)} %collective-permute-done.26.refs_2_) | copy-start | bytes 1572868
  22.6 12.7 %collective-permute-start.15 = (f32[4,64,512]{2,1,0:T(8,128)S(1)}, f32[4,64,512]{2,1,0:T(8,128)S(1)}, u32[]{:S(2)}, u32[]{:S(2)}) collective-permute-start(f32[4,64,512]{2,1,0:T(8,128)S(1)} %pad_maximum_fusion.refs_0_), channel_id=1, source_target_pairs={{0,0},{1,33},{2,18},{3,51},{4,4},{5,37},{6,22},{7,55},{8,8},{9,41}... | collective-permute-start | bytes 1572872 | tf_op jit(solution)/shard_map/ppermute | solution.py:29
  24.5 155.1 %copy-start.22 = (f32[4,64,512]{2,1,0:T(8,128)}, f32[4,64,512]{2,1,0:T(8,128)S(1)}, u32[]{:S(2)}) copy-start(f32[4,64,512]{2,1,0:T(8,128)S(1)} %collective-permute-done.29.refs_4_) | copy-start | bytes 1572868
  24.5 14.5 %collective-permute-start.3 = (f32[4,64,512]{2,1,0:T(8,128)S(1)}, f32[4,64,512]{2,1,0:T(8,128)S(1)}, u32[]{:S(2)}, u32[]{:S(2)}) collective-permute-start(f32[4,64,512]{2,1,0:T(8,128)S(1)} %pad_maximum_fusion.refs_0_), channel_id=1, source_target_pairs={{0,4},{1,5},{2,6},{3,7},{4,8},{5,9},{6,10},{7,11},{8,12},{9,13},{1... | collective-permute-start | bytes 1572872 | tf_op jit(solution)/shard_map/ppermute | solution.py:29
  25.8 153.8 %copy-start.23 = (f32[4,64,512]{2,1,0:T(8,128)}, f32[4,64,512]{2,1,0:T(8,128)S(1)}, u32[]{:S(2)}) copy-start(f32[4,64,512]{2,1,0:T(8,128)S(1)} %collective-permute-done.43.refs_1_) | copy-start | bytes 1572868
  25.8 14.4 %collective-permute-start.7 = (f32[4,64,512]{2,1,0:T(8,128)S(1)}, f32[4,64,512]{2,1,0:T(8,128)S(1)}, u32[]{:S(2)}, u32[]{:S(2)}) collective-permute-start(f32[4,64,512]{2,1,0:T(8,128)S(1)} %pad_maximum_fusion.refs_0_), channel_id=1, source_target_pairs={{0,12},{1,13},{2,14},{3,15},{4,0},{5,1},{6,2},{7,3},{8,4},{9,5},{1... | collective-permute-start | bytes 1572872 | tf_op jit(solution)/shard_map/ppermute | solution.py:29
  27.3 163.8 %copy-start = (f32[4,64,512]{2,1,0:T(8,128)}, f32[4,64,512]{2,1,0:T(8,128)S(1)}, u32[]{:S(2)}) copy-start(f32[4,64,512]{2,1,0:T(8,128)S(1)} %collective-permute-done.24.refs_0_) | copy-start | bytes 1572868
  27.3 13.1 %collective-permute-start = (f32[4,64,512]{2,1,0:T(8,128)S(1)}, f32[4,64,512]{2,1,0:T(8,128)S(1)}, u32[]{:S(2)}, u32[]{:S(2)}) collective-permute-start(f32[4,64,512]{2,1,0:T(8,128)S(1)} %pad_maximum_fusion.refs_0_), channel_id=1, source_target_pairs={{0,1},{1,0},{2,3},{3,2},{4,5},{5,4},{6,7},{7,6},{8,9},{9,8},{10,11... | collective-permute-start | bytes 1572872 | tf_op jit(solution)/shard_map/ppermute | solution.py:29
  32.8 72.7 %copy-start.18 = (f32[4,64,512]{2,1,0:T(8,128)}, f32[4,64,512]{2,1,0:T(8,128)S(1)}, u32[]{:S(2)}) copy-start(f32[4,64,512]{2,1,0:T(8,128)S(1)} %collective-permute-done.1.refs_2_) | copy-start | bytes 1572868
  32.8 15.3 %collective-permute-start.35 = (f32[4,64,512]{2,1,0:T(8,128)S(1)}, f32[4,64,512]{2,1,0:T(8,128)S(1)}, u32[]{:S(2)}, u32[]{:S(2)}) collective-permute-start(f32[4,64,512]{2,1,0:T(8,128)S(1)} %collective-permute-done.34), channel_id=1, source_target_pairs={{0,0},{1,4},{2,6},{3,2},{4,64},{5,68},{6,70},{7,66},{8,1},{9,5},{1... | collective-permute-start | bytes 1572872 | tf_op jit(solution)/shard_map/ppermute | solution.py:29
  35.2 22.1 %collective-permute-start.46 = (f32[4,64,512]{2,1,0:T(8,128)S(1)}, f32[4,64,512]{2,1,0:T(8,128)S(1)}, u32[]{:S(2)}, u32[]{:S(2)}) collective-permute-start(f32[4,64,512]{2,1,0:T(8,128)S(1)} %collective-permute-done.26.refs_2_), channel_id=1, source_target_pairs={{0,4},{1,5},{2,6},{3,7},{4,8},{5,9},{6,10},{7,11},{8,12},{9,13},{1... | collective-permute-start | bytes 1572872 | tf_op jit(solution)/shard_map/ppermute | solution.py:29
  39.1 72.2 %copy-start.19 = (f32[4,64,512]{2,1,0:T(8,128)}, f32[4,64,512]{2,1,0:T(8,128)S(1)}, u32[]{:S(2)}) copy-start(f32[4,64,512]{2,1,0:T(8,128)S(1)} %collective-permute-done.3.refs_4_) | copy-start | bytes 1572868
  39.1 29.6 %collective-permute-start.44 = (f32[4,64,512]{2,1,0:T(8,128)S(1)}, f32[4,64,512]{2,1,0:T(8,128)S(1)}, u32[]{:S(2)}, u32[]{:S(2)}) collective-permute-start(f32[4,64,512]{2,1,0:T(8,128)S(1)} %collective-permute-done.26.refs_2_), channel_id=1, source_target_pairs={{0,1},{1,0},{2,3},{3,2},{4,5},{5,4},{6,7},{7,6},{8,9},{9,8},{10,11... | collective-permute-start | bytes 1572872 | tf_op jit(solution)/shard_map/ppermute | solution.py:29
  40.2 71.2 %copy-start.21 = (f32[4,64,512]{2,1,0:T(8,128)}, f32[4,64,512]{2,1,0:T(8,128)S(1)}, u32[]{:S(2)}) copy-start(f32[4,64,512]{2,1,0:T(8,128)S(1)} %collective-permute-done.7.refs_8_) | copy-start | bytes 1572868
  40.2 28.4 %collective-permute-start.45 = (f32[4,64,512]{2,1,0:T(8,128)S(1)}, f32[4,64,512]{2,1,0:T(8,128)S(1)}, u32[]{:S(2)}, u32[]{:S(2)}) collective-permute-start(f32[4,64,512]{2,1,0:T(8,128)S(1)} %collective-permute-done.29.refs_4_), channel_id=1, source_target_pairs={{0,1},{1,0},{2,3},{3,2},{4,5},{5,4},{6,7},{7,6},{8,9},{9,8},{10,11... | collective-permute-start | bytes 1572872 | tf_op jit(solution)/shard_map/ppermute | solution.py:29
  40.3 31.9 %collective-permute-start.27 = (f32[4,64,512]{2,1,0:T(8,128)S(1)}, f32[4,64,512]{2,1,0:T(8,128)S(1)}, u32[]{:S(2)}, u32[]{:S(2)}) collective-permute-start(f32[4,64,512]{2,1,0:T(8,128)S(1)} %collective-permute-done.26.refs_2_), channel_id=1, source_target_pairs={{0,12},{1,13},{2,14},{3,15},{4,0},{5,1},{6,2},{7,3},{8,4},{9,5},{1... | collective-permute-start | bytes 1572872 | tf_op jit(solution)/shard_map/ppermute | solution.py:29
  48.1 132.4 %copy-start.1 = (f32[4,64,512]{2,1,0:T(8,128)}, f32[4,64,512]{2,1,0:T(8,128)S(1)}, u32[]{:S(2)}) copy-start(f32[4,64,512]{2,1,0:T(8,128)S(1)} %collective-permute-done.35.refs_8_) | copy-start | bytes 1572868
  48.1 24.2 %collective-permute-start.30 = (f32[4,64,512]{2,1,0:T(8,128)S(1)}, f32[4,64,512]{2,1,0:T(8,128)S(1)}, u32[]{:S(2)}, u32[]{:S(2)}) collective-permute-start(f32[4,64,512]{2,1,0:T(8,128)S(1)} %collective-permute-done.29.refs_4_), channel_id=1, source_target_pairs={{0,4},{1,5},{2,6},{3,7},{4,8},{5,9},{6,10},{7,11},{8,12},{9,13},{1... | collective-permute-start | bytes 1572872 | tf_op jit(solution)/shard_map/ppermute | solution.py:29
  57.4 79.7 %copy-start.25 = (f32[4,64,512]{2,1,0:T(8,128)}, f32[4,64,512]{2,1,0:T(8,128)S(1)}, u32[]{:S(2)}) copy-start(f32[4,64,512]{2,1,0:T(8,128)S(1)} %collective-permute-done.46.refs_6_) | copy-start | bytes 1572868
  57.4 16.2 %collective-permute-start.25 = (f32[4,64,512]{2,1,0:T(8,128)S(1)}, f32[4,64,512]{2,1,0:T(8,128)S(1)}, u32[]{:S(2)}, u32[]{:S(2)}) collective-permute-start(f32[4,64,512]{2,1,0:T(8,128)S(1)} %collective-permute-done.24.refs_0_), channel_id=1, source_target_pairs={{0,1},{1,0},{2,3},{3,2},{4,5},{5,4},{6,7},{7,6},{8,9},{9,8},{10,11... | collective-permute-start | bytes 1572872 | tf_op jit(solution)/shard_map/ppermute | solution.py:29
  68.6 13.4 %collective-permute-start.9 = (f32[4,64,512]{2,1,0:T(8,128)S(1)}, f32[4,64,512]{2,1,0:T(8,128)S(1)}, u32[]{:S(2)}, u32[]{:S(2)}) collective-permute-start(f32[4,64,512]{2,1,0:T(8,128)S(1)} %collective-permute-done.1.refs_2_), channel_id=1, source_target_pairs={{0,12},{1,13},{2,14},{3,15},{4,0},{5,1},{6,2},{7,3},{8,4},{9,5},{1... | collective-permute-start | bytes 1572872 | tf_op jit(solution)/shard_map/ppermute | solution.py:29
  68.6 17.7 %collective-permute-start.16 = (f32[4,64,512]{2,1,0:T(8,128)S(1)}, f32[4,64,512]{2,1,0:T(8,128)}, u32[]{:S(2)}, u32[]{:S(2)}) collective-permute-start(f32[4,64,512]{2,1,0:T(8,128)S(1)} %collective-permute-done.15), channel_id=1, source_target_pairs={{0,0},{1,4},{2,6},{3,2},{4,64},{5,68},{6,70},{7,66},{8,1},{9,5},{1... | collective-permute-start | bytes 1572872 | tf_op jit(solution)/shard_map/ppermute | solution.py:29
  72.3 118.8 %copy-start.2 = (f32[4,64,512]{2,1,0:T(8,128)}, f32[4,64,512]{2,1,0:T(8,128)S(1)}, u32[]{:S(2)}) copy-start(f32[4,64,512]{2,1,0:T(8,128)S(1)} %collective-permute-done.27.refs_2_) | copy-start | bytes 1572868
  72.3 22.2 %collective-permute-start.5 = (f32[4,64,512]{2,1,0:T(8,128)S(1)}, f32[4,64,512]{2,1,0:T(8,128)S(1)}, u32[]{:S(2)}, u32[]{:S(2)}) collective-permute-start(f32[4,64,512]{2,1,0:T(8,128)S(1)} %collective-permute-done.1.refs_2_), channel_id=1, source_target_pairs={{0,4},{1,5},{2,6},{3,7},{4,8},{5,9},{6,10},{7,11},{8,12},{9,13},{1... | collective-permute-start | bytes 1572872 | tf_op jit(solution)/shard_map/ppermute | solution.py:29
  72.4 118.8 %copy-start.3 = (f32[4,64,512]{2,1,0:T(8,128)}, f32[4,64,512]{2,1,0:T(8,128)S(1)}, u32[]{:S(2)}) copy-start(f32[4,64,512]{2,1,0:T(8,128)S(1)} %collective-permute-done.30.refs_4_) | copy-start | bytes 1572868
  72.4 31.5 %collective-permute-start.11 = (f32[4,64,512]{2,1,0:T(8,128)S(1)}, f32[4,64,512]{2,1,0:T(8,128)S(1)}, u32[]{:S(2)}, u32[]{:S(2)}) collective-permute-start(f32[4,64,512]{2,1,0:T(8,128)S(1)} %collective-permute-done.3.refs_4_), channel_id=1, source_target_pairs={{0,4},{1,5},{2,6},{3,7},{4,8},{5,9},{6,10},{7,11},{8,12},{9,13},{1... | collective-permute-start | bytes 1572872 | tf_op jit(solution)/shard_map/ppermute | solution.py:29
  73.6 117.6 %copy-start.4 = (f32[4,64,512]{2,1,0:T(8,128)}, f32[4,64,512]{2,1,0:T(8,128)S(1)}, u32[]{:S(2)}) copy-start(f32[4,64,512]{2,1,0:T(8,128)S(1)} %collective-permute-done.25.refs_1_) | copy-start | bytes 1572868
  73.6 31.9 %collective-permute-start.2 = (f32[4,64,512]{2,1,0:T(8,128)S(1)}, f32[4,64,512]{2,1,0:T(8,128)S(1)}, u32[]{:S(2)}, u32[]{:S(2)}) collective-permute-start(f32[4,64,512]{2,1,0:T(8,128)S(1)} %collective-permute-done.1.refs_2_), channel_id=1, source_target_pairs={{0,1},{1,0},{2,3},{3,2},{4,5},{5,4},{6,7},{7,6},{8,9},{9,8},{10,11... | collective-permute-start | bytes 1572872 | tf_op jit(solution)/shard_map/ppermute | solution.py:29
  82.0 26.6 %collective-permute-start.4 = (f32[4,64,512]{2,1,0:T(8,128)S(1)}, f32[4,64,512]{2,1,0:T(8,128)S(1)}, u32[]{:S(2)}, u32[]{:S(2)}) collective-permute-start(f32[4,64,512]{2,1,0:T(8,128)S(1)} %collective-permute-done.3.refs_4_), channel_id=1, source_target_pairs={{0,1},{1,0},{2,3},{3,2},{4,5},{5,4},{6,7},{7,6},{8,9},{9,8},{10,11... | collective-permute-start | bytes 1572872 | tf_op jit(solution)/shard_map/ppermute | solution.py:29
  86.4 24.9 %collective-permute-start.8 = (f32[4,64,512]{2,1,0:T(8,128)S(1)}, f32[4,64,512]{2,1,0:T(8,128)S(1)}, u32[]{:S(2)}, u32[]{:S(2)}) collective-permute-start(f32[4,64,512]{2,1,0:T(8,128)S(1)} %collective-permute-done.7.refs_8_), channel_id=1, source_target_pairs={{0,1},{1,0},{2,3},{3,2},{4,5},{5,4},{6,7},{7,6},{8,9},{9,8},{10,11... | collective-permute-start | bytes 1572872 | tf_op jit(solution)/shard_map/ppermute | solution.py:29
  94.5 16.9 %collective-permute-start.39 = (f32[4,64,512]{2,1,0:T(8,128)S(1)}, f32[4,64,512]{2,1,0:T(8,128)S(1)}, u32[]{:S(2)}, u32[]{:S(2)}) collective-permute-start(f32[4,64,512]{2,1,0:T(8,128)S(1)} %collective-permute-done.35.refs_8_), channel_id=1, source_target_pairs={{0,64},{1,65},{2,66},{3,67},{4,68},{5,69},{6,70},{7,71},{8,72},{9,... | collective-permute-start | bytes 1572872 | tf_op jit(solution)/shard_map/ppermute | solution.py:29
  103.9 14.5 %collective-permute-start.36 = (f32[4,64,512]{2,1,0:T(8,128)S(1)}, f32[4,64,512]{2,1,0:T(8,128)S(1)}, u32[]{:S(2)}, u32[]{:S(2)}) collective-permute-start(f32[4,64,512]{2,1,0:T(8,128)S(1)} %collective-permute-done.35.refs_8_), channel_id=1, source_target_pairs={{0,16},{1,17},{2,18},{3,19},{4,20},{5,21},{6,22},{7,23},{8,24},{9,... | collective-permute-start | bytes 1572872 | tf_op jit(solution)/shard_map/ppermute | solution.py:29
  105.5 74.1 %copy-start.31 = (f32[4,64,512]{2,1,0:T(8,128)}, f32[4,64,512]{2,1,0:T(8,128)S(1)}, u32[]{:S(2)}) copy-start(f32[4,64,512]{2,1,0:T(8,128)S(1)} %collective-permute-done.2.refs_3_) | copy-start | bytes 1572868
  105.5 15.9 %collective-permute-start.37 = (f32[4,64,512]{2,1,0:T(8,128)S(1)}, f32[4,64,512]{2,1,0:T(8,128)S(1)}, u32[]{:S(2)}, u32[]{:S(2)}) collective-permute-start(f32[4,64,512]{2,1,0:T(8,128)S(1)} %collective-permute-done.35.refs_8_), channel_id=1, source_target_pairs={{0,48},{1,49},{2,50},{3,51},{4,52},{5,53},{6,54},{7,55},{8,56},{9,... | collective-permute-start | bytes 1572872 | tf_op jit(solution)/shard_map/ppermute | solution.py:29
  108.6 71.0 %copy-start.32 = (f32[4,64,512]{2,1,0:T(8,128)}, f32[4,64,512]{2,1,0:T(8,128)S(1)}, u32[]{:S(2)}) copy-start(f32[4,64,512]{2,1,0:T(8,128)S(1)} %collective-permute-done.4.refs_5_) | copy-start | bytes 1572868
  108.6 12.8 %collective-permute-start.47 = (f32[4,64,512]{2,1,0:T(8,128)S(1)}, f32[4,64,512]{2,1,0:T(8,128)}, u32[]{:S(2)}, u32[]{:S(2)}) collective-permute-start(f32[4,64,512]{2,1,0:T(8,128)S(1)} %collective-permute-done.46.refs_6_), channel_id=1, source_target_pairs={{0,1},{1,0},{2,3},{3,2},{4,5},{5,4},{6,7},{7,6},{8,9},{9,8},{10,11... | collective-permute-start | bytes 1572872 | tf_op jit(solution)/shard_map/ppermute | solution.py:29
  111.3 13.5 %collective-permute-start.32 = (f32[4,64,512]{2,1,0:T(8,128)S(1)}, f32[4,64,512]{2,1,0:T(8,128)S(1)}, u32[]{:S(2)}, u32[]{:S(2)}) collective-permute-start(f32[4,64,512]{2,1,0:T(8,128)S(1)} %collective-permute-done.27.refs_2_), channel_id=1, source_target_pairs={{0,12},{1,13},{2,14},{3,15},{4,0},{5,1},{6,2},{7,3},{8,4},{9,5},{1... | collective-permute-start | bytes 1572872 | tf_op jit(solution)/shard_map/ppermute | solution.py:29
  111.4 13.4 %collective-permute-start.28 = (f32[4,64,512]{2,1,0:T(8,128)S(1)}, f32[4,64,512]{2,1,0:T(8,128)S(1)}, u32[]{:S(2)}, u32[]{:S(2)}) collective-permute-start(f32[4,64,512]{2,1,0:T(8,128)S(1)} %collective-permute-done.27.refs_2_), channel_id=1, source_target_pairs={{0,1},{1,0},{2,3},{3,2},{4,5},{5,4},{6,7},{7,6},{8,9},{9,8},{10,11... | collective-permute-start | bytes 1572872 | tf_op jit(solution)/shard_map/ppermute | solution.py:29
  118.4 7.9 %collective-permute-start.31 = (f32[4,64,512]{2,1,0:T(8,128)S(1)}, f32[4,64,512]{2,1,0:T(8,128)S(1)}, u32[]{:S(2)}, u32[]{:S(2)}) collective-permute-start(f32[4,64,512]{2,1,0:T(8,128)S(1)} %collective-permute-done.30.refs_4_), channel_id=1, source_target_pairs={{0,1},{1,0},{2,3},{3,2},{4,5},{5,4},{6,7},{7,6},{8,9},{9,8},{10,11... | collective-permute-start | bytes 1572872 | tf_op jit(solution)/shard_map/ppermute | solution.py:29
  121.4 14.8 %collective-permute-start.13 = (f32[4,64,512]{2,1,0:T(8,128)S(1)}, f32[4,64,512]{2,1,0:T(8,128)}, u32[]{:S(2)}, u32[]{:S(2)}) collective-permute-start(f32[4,64,512]{2,1,0:T(8,128)S(1)} %collective-permute-done.9.refs_10_), channel_id=1, source_target_pairs={{0,12},{1,13},{2,14},{3,15},{4,0},{5,1},{6,2},{7,3},{8,4},{9,5},{1... | collective-permute-start | bytes 1572872 | tf_op jit(solution)/shard_map/ppermute | solution.py:29
  121.4 15.7 %collective-permute-start.17 = (f32[4,64,512]{2,1,0:T(8,128)}, f32[4,64,512]{2,1,0:T(8,128)S(1)}, u32[]{:S(2)}, u32[]{:S(2)}) collective-permute-start(f32[4,64,512]{2,1,0:T(8,128)} %collective-permute-done.16.refs_16_), channel_id=1, source_target_pairs={{0,16},{1,17},{2,18},{3,19},{4,20},{5,21},{6,22},{7,23},{8,24},{9,... | collective-permute-start | bytes 1572872 | tf_op jit(solution)/shard_map/ppermute | solution.py:29
  124.8 13.9 %collective-permute-start.20 = (f32[4,64,512]{2,1,0:T(8,128)}, f32[4,64,512]{2,1,0:T(8,128)}, u32[]{:S(2)}, u32[]{:S(2)}) collective-permute-start(f32[4,64,512]{2,1,0:T(8,128)} %collective-permute-done.16.refs_16_), channel_id=1, source_target_pairs={{0,64},{1,65},{2,66},{3,67},{4,68},{5,69},{6,70},{7,71},{8,72},{9,... | collective-permute-start | bytes 1572872 | tf_op jit(solution)/shard_map/ppermute | solution.py:29
  124.8 13.9 %collective-permute-start.10 = (f32[4,64,512]{2,1,0:T(8,128)S(1)}, f32[4,64,512]{2,1,0:T(8,128)S(1)}, u32[]{:S(2)}, u32[]{:S(2)}) collective-permute-start(f32[4,64,512]{2,1,0:T(8,128)S(1)} %collective-permute-done.9.refs_10_), channel_id=1, source_target_pairs={{0,1},{1,0},{2,3},{3,2},{4,5},{5,4},{6,7},{7,6},{8,9},{9,8},{10,11... | collective-permute-start | bytes 1572872 | tf_op jit(solution)/shard_map/ppermute | solution.py:29
  126.3 12.6 %collective-permute-start.6 = (f32[4,64,512]{2,1,0:T(8,128)S(1)}, f32[4,64,512]{2,1,0:T(8,128)S(1)}, u32[]{:S(2)}, u32[]{:S(2)}) collective-permute-start(f32[4,64,512]{2,1,0:T(8,128)S(1)} %collective-permute-done.5.refs_6_), channel_id=1, source_target_pairs={{0,1},{1,0},{2,3},{3,2},{4,5},{5,4},{6,7},{7,6},{8,9},{9,8},{10,11... | collective-permute-start | bytes 1572872 | tf_op jit(solution)/shard_map/ppermute | solution.py:29
  136.2 5.0 %collective-permute-start.12 = (f32[4,64,512]{2,1,0:T(8,128)S(1)}, f32[4,64,512]{2,1,0:T(8,128)S(1)}, u32[]{:S(2)}, u32[]{:S(2)}) collective-permute-start(f32[4,64,512]{2,1,0:T(8,128)S(1)} %collective-permute-done.11.refs_12_), channel_id=1, source_target_pairs={{0,1},{1,0},{2,3},{3,2},{4,5},{5,4},{6,7},{7,6},{8,9},{9,8},{10,11... | collective-permute-start | bytes 1572872 | tf_op jit(solution)/shard_map/ppermute | solution.py:29
  137.1 13.4 %collective-permute-start.41 = (f32[4,64,512]{2,1,0:T(8,128)S(1)}, f32[4,64,512]{2,1,0:T(8,128)S(1)}, u32[]{:S(2)}, u32[]{:S(2)}) collective-permute-start(f32[4,64,512]{2,1,0:T(8,128)S(1)} %collective-permute-done.39.refs_12_), channel_id=1, source_target_pairs={{0,48},{1,49},{2,50},{3,51},{4,52},{5,53},{6,54},{7,55},{8,56},{9,... | collective-permute-start | bytes 1572872 | tf_op jit(solution)/shard_map/ppermute | solution.py:29
  138.7 13.2 %collective-permute-start.40 = (f32[4,64,512]{2,1,0:T(8,128)S(1)}, f32[4,64,512]{2,1,0:T(8,128)S(1)}, u32[]{:S(2)}, u32[]{:S(2)}) collective-permute-start(f32[4,64,512]{2,1,0:T(8,128)S(1)} %collective-permute-done.39.refs_12_), channel_id=1, source_target_pairs={{0,16},{1,17},{2,18},{3,19},{4,20},{5,21},{6,22},{7,23},{8,24},{9,... | collective-permute-start | bytes 1572872 | tf_op jit(solution)/shard_map/ppermute | solution.py:29
  138.8 23.7 %collective-permute-start.38 = (f32[4,64,512]{2,1,0:T(8,128)S(1)}, f32[4,64,512]{2,1,0:T(8,128)S(1)}, u32[]{:S(2)}, u32[]{:S(2)}) collective-permute-start(f32[4,64,512]{2,1,0:T(8,128)S(1)} %collective-permute-done.36.refs_9_), channel_id=1, source_target_pairs={{0,16},{1,17},{2,18},{3,19},{4,20},{5,21},{6,22},{7,23},{8,24},{9,... | collective-permute-start | bytes 1572872 | tf_op jit(solution)/shard_map/ppermute | solution.py:29
  138.9 23.6 %collective-permute-start.33 = (f32[4,64,512]{2,1,0:T(8,128)S(1)}, f32[4,64,512]{2,1,0:T(8,128)S(1)}, u32[]{:S(2)}, u32[]{:S(2)}) collective-permute-start(f32[4,64,512]{2,1,0:T(8,128)S(1)} %collective-permute-done.32.refs_6_), channel_id=1, source_target_pairs={{0,1},{1,0},{2,3},{3,2},{4,5},{5,4},{6,7},{7,6},{8,9},{9,8},{10,11... | collective-permute-start | bytes 1572872 | tf_op jit(solution)/shard_map/ppermute | solution.py:29
  141.2 32.6 %collective-permute-start.19 = (f32[4,64,512]{2,1,0:T(8,128)S(1)}, f32[4,64,512]{2,1,0:T(8,128)}, u32[]{:S(2)}, u32[]{:S(2)}) collective-permute-start(f32[4,64,512]{2,1,0:T(8,128)S(1)} %collective-permute-done.17.refs_17_), channel_id=1, source_target_pairs={{0,16},{1,17},{2,18},{3,19},{4,20},{5,21},{6,22},{7,23},{8,24},{9,... | collective-permute-start | bytes 1572872 | tf_op jit(solution)/shard_map/ppermute | solution.py:29
  150.5 29.1 %collective-permute-start.42 = (f32[4,64,512]{2,1,0:T(8,128)S(1)}, f32[4,64,512]{2,1,0:T(8,128)S(1)}, u32[]{:S(2)}, u32[]{:S(2)}) collective-permute-start(f32[4,64,512]{2,1,0:T(8,128)S(1)} %collective-permute-done.41.refs_14_), channel_id=1, source_target_pairs={{0,48},{1,49},{2,50},{3,51},{4,52},{5,53},{6,54},{7,55},{8,56},{9,... | collective-permute-start | bytes 1572872 | tf_op jit(solution)/shard_map/ppermute | solution.py:29
  152.0 49.7 %collective-permute-start.18 = (f32[4,64,512]{2,1,0:T(8,128)}, f32[4,64,512]{2,1,0:T(8,128)}, u32[]{:S(2)}, u32[]{:S(2)}) collective-permute-start(f32[4,64,512]{2,1,0:T(8,128)} %collective-permute-done.16.refs_16_), channel_id=1, source_target_pairs={{0,48},{1,49},{2,50},{3,51},{4,52},{5,53},{6,54},{7,55},{8,56},{9,... | collective-permute-start | bytes 1572872 | tf_op jit(solution)/shard_map/ppermute | solution.py:29
  162.4 39.3 %collective-permute-start.21 = (f32[4,64,512]{2,1,0:T(8,128)}, f32[4,64,512]{2,1,0:T(8,128)}, u32[]{:S(2)}, u32[]{:S(2)}) collective-permute-start(f32[4,64,512]{2,1,0:T(8,128)} %collective-permute-done.20.refs_20_), channel_id=1, source_target_pairs={{0,16},{1,17},{2,18},{3,19},{4,20},{5,21},{6,22},{7,23},{8,24},{9,... | collective-permute-start | bytes 1572872 | tf_op jit(solution)/shard_map/ppermute | solution.py:29
  162.5 39.2 %collective-permute-start.22 = (f32[4,64,512]{2,1,0:T(8,128)}, f32[4,64,512]{2,1,0:T(8,128)}, u32[]{:S(2)}, u32[]{:S(2)}) collective-permute-start(f32[4,64,512]{2,1,0:T(8,128)} %collective-permute-done.20.refs_20_), channel_id=1, source_target_pairs={{0,48},{1,49},{2,50},{3,51},{4,52},{5,53},{6,54},{7,55},{8,56},{9,... | collective-permute-start | bytes 1572872 | tf_op jit(solution)/shard_map/ppermute | solution.py:29
  173.8 27.9 %collective-permute-start.14 = (f32[4,64,512]{2,1,0:T(8,128)}, f32[4,64,512]{2,1,0:T(8,128)}, u32[]{:S(2)}, u32[]{:S(2)}) collective-permute-start(f32[4,64,512]{2,1,0:T(8,128)} %collective-permute-done.13.refs_14_), channel_id=1, source_target_pairs={{0,1},{1,0},{2,3},{3,2},{4,5},{5,4},{6,7},{7,6},{8,9},{9,8},{10,11... | collective-permute-start | bytes 1572872 | tf_op jit(solution)/shard_map/ppermute | solution.py:29
  180.5 21.2 %collective-permute-start.23 = (f32[4,64,512]{2,1,0:T(8,128)}, f32[4,64,512]{2,1,0:T(8,128)}, u32[]{:S(2)}, u32[]{:S(2)}) collective-permute-start(f32[4,64,512]{2,1,0:T(8,128)} %collective-permute-done.19.refs_19_), channel_id=1, source_target_pairs={{0,64},{1,65},{2,66},{3,67},{4,68},{5,69},{6,70},{7,71},{8,72},{9,... | collective-permute-start | bytes 1572872 | tf_op jit(solution)/shard_map/ppermute | solution.py:29
  (22 other events, 880.5 us)
